TPU v7x, 128 devices: a whole 4x4x4 slice. The times are simulated.
128 devices in a mesh: grid: 32 (over x_hi, z, y), band: 4 (over x_lo, core).
Axes of the slice: x: 4 (x_hi: 2, x_lo: 2; x = x_hi * 2 + x_lo), y: 4, z: 4, core: 2. Of those that a mesh axis runs over, the one named last changes fastest.
Arguments:
- orbitals: float32 [128, 16, 16, 512], P('grid', None, None, 'band'), may hold values from -80 to 80
- projectors: float32 [128, 16, 16, 512], P('grid', None, None, 'band'), may hold values from -0.046875 to 0.046875
- potential: float32 [128, 16, 16], P('grid'), may hold values from 0.3 to 3
Outputs:
- updated_orbitals: float32 [128, 16, 16, 512], P('grid', None, None, 'band')
- rayleigh_quotients: float32 [3, 512], P(None, 'band')
- residual_norms: float32 [3, 512], P(None, 'band')
All inputs are finite; a program needn't handle non-finite values.
Results may differ from a plain program's by a relative error of at most 0.00012.
Values sent between devices are 32-bit elements; how exact they have to be, the bound alone decides.
No kernel may reach another device: no remote copies, remote signals or barrier semaphores. Data moves between devices by JAX's collectives and lax.ppermute only.
A program may use at most 128 MiB of HBM per device.

v0:
```python
import jax
import jax.numpy as jnp
from jax import lax
from jax.experimental import pallas as pl
from jax.experimental.pallas import tpu as pltpu
from jax.sharding import Mesh
from jax.sharding import PartitionSpec as P

ITERS = 3
BAND = ("band_0", "band_1")
CHIPS = ("grid", "band_0")
EVERY = ("grid", "band_0", "band_1")
BLOCK = 128
TILE = 8
HALF = 64
LINES = 2

STENCIL = (-205.0 / 72.0, 8.0 / 5.0, -1.0 / 5.0, 8.0 / 315.0, -1.0 / 560.0)
STEP_LENGTH = 0.25
NORM_EPS = 1e-06
WHOLE = pl.BlockSpec(memory_space=pltpu.VMEM)


def split(x):
    high = x.astype(jnp.bfloat16)
    return high, (x - high.astype(jnp.float32)).astype(jnp.bfloat16)


def dot(left, right, sides):
    (lh, ll), (rh, rl) = split(left), split(right)

    def once(a, b):
        return lax.dot_general(
            a, b, ((sides[:1], sides[1:]), ((), ())), preferred_element_type=jnp.float32
        )

    return once(lh, rl) + once(ll, rh) + once(lh, rh)


def row_of(tile, j):
    return jnp.broadcast_to(tile[j:j + 1, :], tile.shape)


def lane_of(tile, j):
    return jnp.broadcast_to(tile[:, j:j + 1], tile.shape)


def inverse_factor(tiles):
    count = len(tiles)
    lane = lax.broadcasted_iota(jnp.int32, tiles[0].shape, 1)
    sub = lax.broadcasted_iota(jnp.int32, tiles[0].shape, 0)
    tiles = list(tiles)
    head = [lane_of(tiles[0], j) for j in range(TILE)]
    for p in range(count):
        base = TILE * p
        inside = (lane >= base) & (lane < base + TILE)
        own = jnp.where(inside, (lane == base + sub).astype(jnp.float32), tiles[p])
        ahead = p + 1 < count
        if ahead:
            coming = [lane_of(tiles[p + 1], base + TILE + j) for j in range(TILE)]
        rows, crosses = [], []
        for j in range(TILE):
            scale = lax.rsqrt(row_of(head[j], j))
            row = row_of(own, j) * scale
            column = jnp.where(sub > j, head[j] * scale, 0.0)
            own = jnp.where(sub == j, row, own - column * row)
            cross = [None] * TILE
            for k in range(j + 1, TILE):
                cross[k] = row_of(head[k], j) * scale
                head[k] = head[k] - column * cross[k]
                cross[k] = cross[k] * scale
            rows.append(row * scale)
            crosses.append(cross)
            if ahead:
                if j == 0:
                    parts = [lane_of(tiles[p + 1], base + k) for k in range(TILE)]
                    following = jnp.where(inside, 0.0, tiles[p + 1])
                following = following - parts[j] * rows[j]
                for k in range(j + 1, TILE):
                    parts[k] = parts[k] - parts[j] * crosses[j][k]
                scaled = parts[j] * (scale * scale)
                for k in range(TILE):
                    coming[k] = coming[k] - scaled * row_of(parts[j], k)
        tiles[p] = jnp.where((lane < base + TILE) | (lane >= TILE * count), own, 0.0)
        if ahead:
            tiles[p + 1] = following
            head = coming
        for t in range(p + 2, count):
            parts = [lane_of(tiles[t], base + j) for j in range(TILE)]
            tile = jnp.where(inside, 0.0, tiles[t])
            for j in range(TILE):
                tile = tile - parts[j] * rows[j]
                for k in range(j + 1, TILE):
                    parts[k] = parts[k] - parts[j] * crosses[j][k]
            tiles[t] = tile
    return tiles


def pairs_of(blocks):
    return [(i, j) for i in range(blocks) for j in range(i, blocks)]


def cut(x, b):
    return x[:, BLOCK * b : BLOCK * (b + 1)]


def rows_at(ref, at):
    return ref[BLOCK * at : BLOCK * (at + 1), :]


def block_of(core, mine_ref, other_ref, at):
    half = mine_ref.shape[0] // BLOCK
    mine, other = rows_at(mine_ref, at % half), rows_at(other_ref, at % half)
    here = jnp.full(mine.shape, core, jnp.int32) == at // half
    return jnp.where(here, mine, other)


def factorize(x_ref):
    blocks = x_ref.shape[0] // BLOCK
    for i in range(1, blocks):
        x_ref[BLOCK * i : BLOCK * (i + 1), : BLOCK * i] = jnp.zeros((BLOCK, BLOCK * i), jnp.float32)
    block_row = lax.broadcasted_iota(jnp.int32, (BLOCK, BLOCK), 0)
    block_lane = lax.broadcasted_iota(jnp.int32, (BLOCK, BLOCK), 1)

    def step(k, carry):
        first = pl.multiple_of(k * BLOCK, BLOCK)
        here = pl.ds(first, BLOCK)

        def part(h, carry):
            top = first + HALF * h
            rows = [pl.ds(pl.multiple_of(top + TILE * t, TILE), TILE) for t in range(HALF // TILE)]
            tiles = inverse_factor([pltpu.roll(x_ref[r, here], HALF * h, 1) for r in rows])
            for r, tile in zip(rows, tiles):
                x_ref[r, here] = pltpu.roll(tile, HALF * h, 1)

            @pl.when(h == 0)
            def _():
                upper = x_ref[pl.ds(first, HALF), here]
                below = pl.ds(pl.multiple_of(first + HALF, HALF), HALF)
                change = dot(upper, upper, (0, 0))[HALF:, :]
                lane = lax.broadcasted_iota(jnp.int32, change.shape, 1)
                x_ref[below, here] = jnp.where(lane < HALF, 0.0, x_ref[below, here]) - change

            return carry

        lax.fori_loop(0, 2, part, 0)
        own = jnp.where((block_row < HALF) & (block_lane >= HALF), 0.0, x_ref[here, here])
        x_ref[here, here] = jnp.where(block_row == block_lane, 1.0, 0.0)
        x_ref[here, :] = dot(own, x_ref[here, :], (1, 0))

        def update(i, carry):
            there = pl.ds(pl.multiple_of(i * BLOCK, BLOCK), BLOCK)
            x_ref[there, here] = jnp.zeros((BLOCK, BLOCK), jnp.float32)
            x_ref[there, :] = x_ref[there, :] - dot(x_ref[here, there], x_ref[here, :], (0, 0))
            return carry

        return lax.fori_loop(k + 1, blocks, update, carry)

    lax.fori_loop(0, blocks, step, 0)
    for i in range(blocks - 1):
        x_ref[BLOCK * i : BLOCK * (i + 1), BLOCK * (i + 1) :] = jnp.zeros(
            (BLOCK, BLOCK * (blocks - 1 - i)), jnp.float32
        )


def first_factor_kernel(core_ref, mine_ref, other_ref, x_ref):
    blocks = x_ref.shape[0] // BLOCK
    for at, (i, j) in enumerate(pairs_of(blocks)):
        x_ref[BLOCK * i : BLOCK * (i + 1), BLOCK * j : BLOCK * (j + 1)] = block_of(
            core_ref[0], mine_ref, other_ref, at
        )
    factorize(x_ref)


def squared_of(rayleigh, energy, weight):
    return jnp.maximum(energy - 2.0 * rayleigh * rayleigh + rayleigh * rayleigh * weight, 0.0)


def length_of(squared):
    return STEP_LENGTH / jnp.sqrt(squared + NORM_EPS)


def factor_kernel(core_ref, mine_ref, other_ref, x_ref, stats_ref):
    blocks = x_ref.shape[0] // BLOCK
    pairs = pairs_of(blocks)
    spot = lax.broadcasted_iota(jnp.int32, (BLOCK, BLOCK), 0) == lax.broadcasted_iota(
        jnp.int32, (BLOCK, BLOCK), 1
    )

    def block(at):
        return block_of(core_ref[0], mine_ref, other_ref, at)

    weights = block(2 * len(pairs) + blocks * blocks)[:TILE]
    parts = {0: [], 1: []}
    for b in range(blocks):
        at = pairs.index((b, b))
        products, energies = block(at), block(len(pairs) + at)
        weight = jnp.broadcast_to(weights[b : b + 1], (BLOCK, BLOCK))
        for axis in (0, 1):
            rayleigh, energy, share = (
                jnp.sum(jnp.where(spot, m, 0.0), axis=axis, keepdims=True)
                for m in (products, energies, weight)
            )
            squared = squared_of(rayleigh, energy, share)
            length = length_of(squared)
            parts[axis].append((1.0 + rayleigh * length, length, share))
            if axis == 0:
                stats_ref[b : b + 1, :] = rayleigh
                stats_ref[blocks + b : blocks + b + 1, :] = squared
    for at, (i, j) in enumerate(pairs):
        a_i, d_i, _ = parts[1][i]
        a_j, d_j, share = parts[0][j]
        value = (d_i * d_j) * block(len(pairs) + at) - (a_i * d_j + d_i * a_j) * block(at)
        if i == j:
            value = value + jnp.where(spot, a_j * a_j * share, 0.0)
        x_ref[BLOCK * i : BLOCK * (i + 1), BLOCK * j : BLOCK * (j + 1)] = value
    factorize(x_ref)


def joined(ref):
    return jnp.concatenate([ref[b] for b in range(ref.shape[0])], axis=1)


def share_out(core, packed_ref, mine_ref, other_ref):
    half = mine_ref.shape[0]
    mine_ref[...] = packed_ref[pl.ds(pl.multiple_of(core * half, TILE), half), :]
    other_ref[...] = packed_ref[pl.ds(pl.multiple_of((1 - core) * half, TILE), half), :]


def write_pairs(left, right, at, packed_ref):
    blocks = left.shape[1] // BLOCK
    for i in range(blocks):
        row = dot(cut(left, i), right[:, BLOCK * i :], (0, 0))
        for j in range(blocks - i):
            packed_ref[BLOCK * at : BLOCK * (at + 1), :] = cut(row, j)
            at += 1
    return at


def write_coupling(xi, v, at, packed_ref):
    blocks = v.shape[1] // BLOCK
    c = dot(xi, v, (0, 0))
    for j in range(blocks):
        packed_ref[BLOCK * at : BLOCK * (at + blocks), :] = cut(c, j)
        at += blocks
    return at


def gram_kernel(core_ref, v_ref, xi_ref, mine_ref, other_ref, packed_ref):
    v = joined(v_ref)
    at = write_pairs(v, v, 0, packed_ref)
    write_coupling(joined(xi_ref), v, at, packed_ref)
    share_out(core_ref[0], packed_ref, mine_ref, other_ref)


def totals_of(core, mine_ref, other_ref):
    mine = jnp.sum(mine_ref[...], axis=0)
    other = jnp.sum(other_ref[...], axis=0)
    first = jnp.full(mine.shape, core, jnp.int32) == 0
    return jnp.concatenate([jnp.where(first, mine, other), jnp.where(first, other, mine)], axis=0)


def along_lanes(rows, at, blocks):
    return jnp.concatenate([rows[at + b : at + b + 1] for b in range(blocks)], axis=1)


def last_kernel(core_ref, own_ref, near_ref, across_ref, far_ref, here_ref, there_ref, v_ref, stats_ref):
    planes, rows = own_ref.shape[1:3]
    totals = totals_of(core_ref[0], here_ref, there_ref)
    blocks = totals.shape[0] // 3
    rayleigh, energy, weight = (totals[blocks * k : blocks * (k + 1)] for k in range(3))
    stats_ref[:blocks, :] = rayleigh
    stats_ref[blocks:, :] = squared_of(rayleigh, energy, weight)
    rayleigh = stats_ref[pl.ds(core_ref[1], 1), :]
    length = length_of(stats_ref[pl.ds(blocks + core_ref[1], 1), :])
    for away, ref in enumerate((own_ref, near_ref, across_ref, far_ref)):
        first_row = rows * lax.rem(core_ref[1] + core_ref[2] + blocks - away, blocks)
        for z in range(planes):
            for x in range(rows):
                vp = ref[0, z, x]
                v_ref[z, first_row + x] = vp - (ref[1, z, x] - rayleigh * vp) * length


def local_part(v_ref, around, p_ref, u_ref):
    below_ref, above_ref, left_ref, right_ref = around
    blocks, planes, rows, columns, _ = v_ref.shape
    along_z = [(ref, z) for ref in (below_ref, v_ref, above_ref) for z in range(planes)]
    along_x = [(ref, x) for ref in (left_ref, v_ref, right_ref) for x in range(rows)]

    def one(b, carry):
        for z in range(planes):
            for x in range(rows):
                centre = v_ref[b, z, x]
                total = 3.0 * STENCIL[0] * centre
                for d in range(1, 5):
                    group = pltpu.roll(centre, d, 0) + pltpu.roll(centre, columns - d, 0)
                    for way in (d, -d):
                        ref, at = along_z[planes + z + way]
                        group = group + ref[b, at, x]
                        ref, at = along_x[rows + x + way]
                        group = group + ref[b, z, at]
                    total = total + STENCIL[d] * group
                u_ref[b, z, x] = p_ref[z, x] * centre - 0.5 * total
        return carry

    lax.fori_loop(0, blocks, one, 0)


def flat_lanes(ref):
    blocks, planes, rows, columns, lanes = ref.shape
    return jnp.concatenate(
        [ref[b].reshape(planes * rows * columns, lanes) for b in range(blocks)], axis=1
    )


def fill_coupling(c_ref, core, mine_ref, other_ref, at):
    blocks = c_ref.shape[1] // BLOCK
    for j in range(blocks):
        for i in range(blocks):
            c_ref[BLOCK * i : BLOCK * (i + 1), BLOCK * j : BLOCK * (j + 1)] = block_of(
                core, mine_ref, other_ref, at
            )
            at += 1


def transformed(v, x):
    middle = x.shape[0] // 2
    return jnp.concatenate(
        [dot(v[:, :middle], x[:middle, :middle], (1, 1)), dot(v, x[middle:, :], (1, 1))], axis=1
    )


def line_sums(product):
    total = jnp.sum(product, axis=0, keepdims=True)
    return [cut(total, b) for b in range(product.shape[1] // BLOCK)]


def finish(core, band, vp, w, xi, vp_ref, w_ref, packed_ref, mine_ref, other_ref):
    blocks = vp.shape[1] // BLOCK
    if packed_ref is None:
        for b in range(blocks):
            away = lax.rem(b + blocks - band, blocks)
            vp_ref[away, 0] = cut(vp, b).reshape(vp_ref.shape[2:])
            vp_ref[away, 1] = cut(w, b).reshape(vp_ref.shape[2:])
        lines = line_sums(vp * w) + line_sums(w * w) + line_sums(vp * vp)
        half = len(lines) // 2
        first, second = (jnp.concatenate(part, axis=0) for part in (lines[:half], lines[half:]))
        front = jnp.full(first.shape, core, jnp.int32) == 0
        mine_ref[...] = jnp.where(front, first, second)
        other_ref[...] = jnp.where(front, second, first)
        return
    for b in range(blocks):
        vp_ref[b] = cut(vp, b)
        w_ref[b] = cut(w, b).reshape(w_ref.shape[1:])
    at = write_pairs(vp, w, 0, packed_ref)
    at = write_pairs(w, w, at, packed_ref)
    at = write_coupling(xi, w, at, packed_ref)
    packed_ref[BLOCK * at :, :] = jnp.zeros((packed_ref.shape[0] - BLOCK * at, BLOCK), jnp.float32)
    packed_ref[BLOCK * at : BLOCK * at + blocks, :] = jnp.concatenate(line_sums(vp * vp), axis=0)
    share_out(core, packed_ref, mine_ref, other_ref)


def first_transform_kernel(
    core_ref, x_ref, in_mine_ref, in_other_ref, v_ref, below_ref, above_ref, left_ref, right_ref, p_ref,
    xi_ref, vp_ref, w_ref, mine_ref, other_ref, c_ref, u_ref, packed_ref,
):
    blocks = v_ref.shape[0]
    at = len(pairs_of(blocks))
    fill_coupling(c_ref, core_ref[0], in_mine_ref, in_other_ref, at)
    local_part(v_ref, (below_ref, above_ref, left_ref, right_ref), p_ref, u_ref)
    v = flat_lanes(v_ref)
    xi = joined(xi_ref)
    z = flat_lanes(u_ref) - dot(xi, c_ref[...], (1, 0))
    both = transformed(jnp.concatenate([v, z], axis=0), x_ref[...])
    finish(
        core_ref[0], core_ref[1], both[: v.shape[0]], both[v.shape[0] :], xi, vp_ref, w_ref, packed_ref, mine_ref,
        other_ref,
    )


def stepped(vp, w, y, stats, blocks):
    rayleigh = along_lanes(stats, 0, blocks)
    length = length_of(along_lanes(stats, blocks, blocks))
    return vp - (w - rayleigh * vp) * length, w - (y - rayleigh * w) * length


def last_transform_kernel(*refs):
    outs = 14
    transform_kernel(*refs[:outs], None, *refs[outs:], None)


def transform_kernel(
    core_ref, x_ref, stats_ref, in_mine_ref, in_other_ref, old_ref, v_ref, below_ref, above_ref, left_ref,
    right_ref, p_ref, xi_ref, vp_ref, w_ref, mine_ref, other_ref, c_ref, u_ref, packed_ref,
):
    blocks = v_ref.shape[0]
    at = 2 * len(pairs_of(blocks))
    fill_coupling(c_ref, core_ref[0], in_mine_ref, in_other_ref, at)
    local_part(v_ref, (below_ref, above_ref, left_ref, right_ref), p_ref, u_ref)
    xi = joined(xi_ref)
    y = flat_lanes(u_ref) - dot(xi, c_ref[...], (1, 0))
    v, z = stepped(joined(old_ref), flat_lanes(v_ref), y, stats_ref[...], blocks)
    both = transformed(jnp.concatenate([v, z], axis=0), x_ref[...])
    finish(
        core_ref[0], core_ref[1], both[: v.shape[0]], both[v.shape[0] :], xi, vp_ref, w_ref, packed_ref, mine_ref,
        other_ref,
    )


def ring(count, by):
    return [(i, (i + by) % count) for i in range(count)]


def turn():
    far = lax.axis_index("grid") // (lax.axis_size("grid") // 2)
    return far * (lax.axis_size(BAND) // 2)


def slab_ring(by):
    slabs, quarters = lax.axis_size("grid"), lax.axis_size(BAND)

    def pair(g, b):
        there = (g + by) % slabs
        crosses = g // (slabs // 2) != there // (slabs // 2)
        return g * quarters + b, there * quarters + (b + crosses * (quarters // 2)) % quarters

    return [pair(g, b) for g in range(slabs) for b in range(quarters)]


def neighbours(v):
    near = lax.axis_size(BAND)
    return (
        lax.ppermute(v, EVERY, slab_ring(1)),
        lax.ppermute(v, EVERY, slab_ring(-1)),
        lax.ppermute(v, BAND, ring(near, 1)),
        lax.ppermute(v, BAND, ring(near, -1)),
    )


def swapped(x):
    return lax.ppermute(x, "band_1", ring(lax.axis_size("band_1"), 1))


def exchange(pieces):
    return lax.all_to_all(pieces, CHIPS, split_axis=0, concat_axis=0, tiled=True)


def from_every_chip(x):
    count = lax.axis_size(CHIPS)
    copies = jnp.broadcast_to(x, (count, *x.shape)).reshape(count * x.shape[0], *x.shape[1:])
    return exchange(copies)


def total_everywhere(mine, other):
    rows, lanes = mine.shape
    count = lax.axis_size(CHIPS)
    pieces = (mine + swapped(other)).reshape(rows // LINES, LINES, lanes)
    arrived = exchange(pieces)
    total = arrived.reshape(count, rows // LINES // count, LINES, lanes).sum(axis=0)
    half = from_every_chip(total).reshape(rows, lanes)
    return half, swapped(half)


def to_cells(*fields):
    count = lax.axis_size(BAND)
    z, x, y, lanes = fields[0].shape
    pieces = jnp.stack([f.reshape(z, 2, count // 2, x // count, y, lanes) for f in fields])
    pieces = jnp.where(turn() == 0, pieces, pieces[:, :, ::-1])
    pieces = pieces.reshape(len(fields), z, count, x // count, y, lanes)
    pieces = lax.all_to_all(jnp.moveaxis(pieces, 2, 0), BAND, split_axis=0, concat_axis=0, tiled=True)
    return [pieces[:, at] for at in range(len(fields))]


def call(kernel, shapes, *args, scratch=(), flops=2_000_000_000, room=32):
    place = jnp.stack([lax.axis_index("band_1"), lax.axis_index(BAND), turn()]).astype(jnp.int32)
    return pl.pallas_call(
        kernel,
        out_shape=[jax.ShapeDtypeStruct(s, jnp.float32) for s in shapes],
        in_specs=[pl.BlockSpec(memory_space=pltpu.SMEM)] + [WHOLE] * len(args),
        out_specs=[WHOLE] * len(shapes),
        scratch_shapes=[pltpu.VMEM(s, jnp.float32) for s in scratch],
        compiler_params=pltpu.CompilerParams(vmem_limit_bytes=room << 20),
        cost_estimate=pl.CostEstimate(
            flops=flops, bytes_accessed=4 * sum(a.size for a in args), transcendentals=0
        ),
    )(place, *args)


def local(orbitals, projectors, potential):
    v, xi = to_cells(orbitals, projectors)
    full = v.shape
    blocks, planes, rows, columns, lanes = full
    flat = (blocks, planes * rows * columns, lanes)
    total = blocks * lanes
    square = (total, total)
    xi = xi.reshape(flat)
    band = lax.axis_index(BAND)
    own = lax.dynamic_slice_in_dim(potential, (band + turn()) % blocks * rows, rows, 1)
    own = jnp.broadcast_to(own[..., None], (planes, rows, columns, lanes))
    pairs = len(pairs_of(blocks))

    def packed(count):
        return (BLOCK * count, BLOCK), (BLOCK * count // 2, BLOCK)

    small, small_half = packed(pairs + blocks * blocks)
    large, large_half = packed(2 * pairs + blocks * blocks + 2)
    sums = (3 * blocks // 2, BLOCK)
    stats_shape = (2 * blocks, BLOCK)
    stats_list = []
    around = neighbours(v)
    mine, other = total_everywhere(*call(gram_kernel, [small_half] * 2, v.reshape(flat), xi, scratch=[small]))
    (x,) = call(first_factor_kernel, [square], mine, other, flops=20_000_000_000, room=16)
    vp, w, mine, other = call(
        first_transform_kernel, [flat, full, large_half, large_half], x, mine, other, v, *around, own, xi,
        scratch=[square, full, large],
    )
    for iteration in range(1, ITERS):
        around = neighbours(w)
        mine, other = total_everywhere(mine, other)
        x, stats = call(factor_kernel, [square, stats_shape], mine, other, flops=20_000_000_000, room=16)
        stats_list.append(stats)
        given = (x, stats, mine, other, vp, w, *around, own, xi)
        if iteration < ITERS - 1:
            vp, w, mine, other = call(
                transform_kernel, [flat, full, large_half, large_half], *given,
                scratch=[square, full, large],
            )
    both = (blocks, 2, planes, rows, columns, lanes)
    parts, mine, other = call(
        last_transform_kernel, [both, sums, sums], *given, scratch=[square, full]
    )
    parts = [parts[0]] + [lax.ppermute(parts[k], BAND, ring(blocks, k)) for k in range(1, blocks)]
    lines = (mine + swapped(other)).reshape(-1, LINES, lanes)
    here = from_every_chip(lines)
    here = here.reshape(lax.axis_size(CHIPS), *sums)
    v, stats = call(
        last_kernel, [(planes, blocks * rows, columns, lanes), stats_shape], *parts, here, swapped(here)
    )
    stats_list.append(stats)
    stats = jnp.stack(stats_list).reshape(ITERS, 2, blocks, lanes)
    stats = lax.dynamic_slice_in_dim(stats, band, 1, 2)[:, :, 0]
    return (v, stats[:, 0], jnp.sqrt(stats[:, 1]))


def solution(mesh):
    finer = Mesh(mesh.devices.reshape(mesh.shape["grid"], 2, 2), ("grid", "band_0", "band_1"))
    placed = (P("grid", None, None, BAND), P("grid", None, None, BAND), P("grid", None, None))
    return jax.shard_map(
        local,
        mesh=finer,
        in_specs=placed,
        out_specs=(P("grid", None, None, BAND), P(None, BAND), P(None, BAND)),
        check_vma=False,
    )
```

profile of v0, /device:TPU:0, one launch (start us, length us, event | category | flops | bytes accessed | tf_op | source)
XLA Modules:
  0.0 293.2 jit_solution(13000754668608860148)
XLA Ops:
  0.7 1.3 pad_maximum_fusion
  2.1 1.1 reverse_select_fusion
  3.2 3.5 %all-to-all-start = ((f32[4,2,4,4,16,128]{5,4,3,2,1,0:T(8,128)}), f32[4,2,4,4,16,128]{5,4,3,2,1,0:T(8,128)S(1)}, u32[]{:S(2)}, u32[]{:S(2)}) async-start(f32[4,2,4,4,16,128]{5,4,3,2,1,0:T(8,128)} %bitcast.6), calls=%async_computation | async-start | bytes 2097152 | tf_op jit(solution)/shard_map/all_to_all | solution.py:470
  6.8 14.3 %all-to-all-done = f32[4,2,4,4,16,128]{5,4,3,2,1,0:T(8,128)S(1)} async-done(((f32[4,2,4,4,16,128]{5,4,3,2,1,0:T(8,128)}), f32[4,2,4,4,16,128]{5,4,3,2,1,0:T(8,128)S(1)}, u32[]{:S(2)}, u32[]{:S(2)}) %all-to-all-start) | async-done | bytes 1048608 | tf_op jit(solution)/shard_map/all_to_all | solution.py:470
  21.3 1.6 shard_map.58
  22.9 2.4 collective-permute-done
  25.4 27.6 %all_to_all.40 = f32[832,2,128]{2,1,0:T(2,128)S(1)} all-to-all(f32[832,2,128]{2,1,0:T(2,128)S(1)} %bitcast.69), channel_id=1, replica_groups=mesh['grid'=32,'band_0'=2,'band_1'=2] {'grid','band_0'}, dimensions={0} | all-to-all | bytes 1703936 | tf_op jit(solution)/shard_map/all_to_all | solution.py:445
  53.5 20.2 %all_to_all.41 = f32[832,2,128]{2,1,0:T(2,128)S(1)} all-to-all(f32[832,2,128]{2,1,0:T(2,128)S(1)} %bitcast.71), channel_id=1, replica_groups=mesh['grid'=32,'band_0'=2,'band_1'=2] {'grid','band_0'}, dimensions={0} | all-to-all | bytes 1703936 | tf_op jit(solution)/shard_map/all_to_all | solution.py:445
  74.5 3.3 %collective-permute-start.3 = (f32[4,4,4,16,128]{4,3,2,1,0:T(8,128)S(1)}, f32[4,4,4,16,128]{4,3,2,1,0:T(8,128)S(1)}, u32[]{:S(2)}, u32[]{:S(2)}) collective-permute-start(f32[4,4,4,16,128]{4,3,2,1,0:T(8,128)S(1)} %get-tuple-element.45.v_ref), channel_id=1, source_target_pairs={{0,126},{1,127},{2,124},{3,125},{4,0},{5,1},{6,2},{7,3},{8,4},{9,5... | collective-permute-start | bytes 1572872 | tf_op jit(solution)/shard_map/ppermute | solution.py:434
  77.8 15.8 %shard_map.59.x_ref = f32[512,512]{1,0:T(8,128)S(1)} custom-call(s32[3]{0:T(128)S(1)} %pad_add_fusion.core_ref.refs_0_, f32[1664,128]{1,0:T(8,128)S(1)} %bitcast.53, f32[1664,128]{1,0:T(8,128)S(1)} %collective-permute-done.1.other_ref.in_other_ref), custom_call_target="tpu_custom_call" | custom-call | flops 20000000000 | bytes 1703936 | tf_op jit(solution)/shard_map/pallas_call | solution.py:476
  93.6 3.9 %collective-permute-done.2.below_ref = f32[4,4,4,16,128]{4,3,2,1,0:T(8,128)S(1)} collective-permute-done((f32[4,4,4,16,128]{4,3,2,1,0:T(8,128)S(1)}, f32[4,4,4,16,128]{4,3,2,1,0:T(8,128)S(1)}, u32[]{:S(2)}, u32[]{:S(2)}) %collective-permute-start.2) | collective-permute-done | bytes 524320 | tf_op jit(solution)/shard_map/ppermute | solution.py:433
  97.6 4.5 %shard_map.60 = (f32[4,256,128]{2,1,0:T(8,128)S(1)}, f32[4,4,4,16,128]{4,3,2,1,0:T(8,128)S(1)}, f32[2432,128]{1,0:T(8,128)S(1)}, f32[2432,128]{1,0:T(8,128)S(1)}) custom-call(s32[3]{0:T(128)S(1)} %pad_add_fusion.core_ref.refs_0_, f32[512,512]{1,0:T(8,128)S(1)} %shard_map.59.x_ref, f32[1664,128]{1,0:T(8,128)S(1)} %bitcast.54, ...), custom_call_target="tpu_custom_call" | custom-call | flops 2000000000 | bytes 6029312 | tf_op jit(solution)/shard_map/pallas_call | solution.py:476
  102.2 2.9 collective-permute-done.6
  105.3 25.5 %all_to_all.42 = f32[1216,2,128]{2,1,0:T(2,128)S(1)} all-to-all(f32[1216,2,128]{2,1,0:T(2,128)S(1)} %bitcast.63), channel_id=1, replica_groups=mesh['grid'=32,'band_0'=2,'band_1'=2] {'grid','band_0'}, dimensions={0} | all-to-all | bytes 2490368 | tf_op jit(solution)/shard_map/all_to_all | solution.py:445
  131.6 25.2 %all_to_all.43 = f32[1216,2,128]{2,1,0:T(2,128)S(1)} all-to-all(f32[1216,2,128]{2,1,0:T(2,128)S(1)} %bitcast.65), channel_id=1, replica_groups=mesh['grid'=32,'band_0'=2,'band_1'=2] {'grid','band_0'}, dimensions={0} | all-to-all | bytes 2490368 | tf_op jit(solution)/shard_map/all_to_all | solution.py:445
  157.4 3.6 %collective-permute-start.9 = (f32[4,4,4,16,128]{4,3,2,1,0:T(8,128)S(1)}, f32[4,4,4,16,128]{4,3,2,1,0:T(8,128)S(1)}, u32[]{:S(2)}, u32[]{:S(2)}) collective-permute-start(f32[4,4,4,16,128]{4,3,2,1,0:T(8,128)S(1)} %copy-done.2), channel_id=1, source_target_pairs={{0,126},{1,127},{2,124},{3,125},{4,0},{5,1},{6,2},{7,3},{8,4},{9,5... | collective-permute-start | bytes 1572872 | tf_op jit(solution)/shard_map/ppermute | solution.py:434
  161.0 16.4 %shard_map.61 = (f32[512,512]{1,0:T(8,128)S(1)}, f32[8,128]{1,0:T(8,128)S(1)}) custom-call(s32[3]{0:T(128)S(1)} %pad_add_fusion.core_ref.refs_0_, f32[2432,128]{1,0:T(8,128)S(1)} %bitcast.50, f32[2432,128]{1,0:T(8,128)S(1)} %collective-permute-done.7.other_ref.in_other_ref), custom_call_target="tpu_custom_call" | custom-call | flops 20000000000 | bytes 2490368 | tf_op jit(solution)/shard_map/pallas_call | solution.py:476
  177.5 3.4 %collective-permute-done.8.below_ref = f32[4,4,4,16,128]{4,3,2,1,0:T(8,128)S(1)} collective-permute-done((f32[4,4,4,16,128]{4,3,2,1,0:T(8,128)S(1)}, f32[4,4,4,16,128]{4,3,2,1,0:T(8,128)S(1)}, u32[]{:S(2)}, u32[]{:S(2)}) %collective-permute-start.8) | collective-permute-done | bytes 524320 | tf_op jit(solution)/shard_map/ppermute | solution.py:433
  180.8 4.5 %shard_map.62 = (f32[4,256,128]{2,1,0:T(8,128)S(1)}, f32[4,4,4,16,128]{4,3,2,1,0:T(8,128)S(1)}, f32[2432,128]{1,0:T(8,128)S(1)}, f32[2432,128]{1,0:T(8,128)S(1)}) custom-call(s32[3]{0:T(128)S(1)} %pad_add_fusion.core_ref.refs_0_, f32[512,512]{1,0:T(8,128)S(1)} %get-tuple-element.26.x_ref, f32[8,128]{1,0:T(8,128)S(1)} %get-tuple-element.27.stats_ref, ...), custom_call_target="tpu_custom_call" | custom-call | flops 2000000000 | bytes 7344128 | tf_op jit(solution)/shard_map/pallas_call | solution.py:476
  185.4 2.9 collective-permute-done.12
  188.5 26.1 %all_to_all.44 = f32[1216,2,128]{2,1,0:T(2,128)S(1)} all-to-all(f32[1216,2,128]{2,1,0:T(2,128)S(1)} %bitcast.64), channel_id=1, replica_groups=mesh['grid'=32,'band_0'=2,'band_1'=2] {'grid','band_0'}, dimensions={0} | all-to-all | bytes 2490368 | tf_op jit(solution)/shard_map/all_to_all | solution.py:445
  215.4 25.0 %all_to_all.45 = f32[1216,2,128]{2,1,0:T(2,128)S(1)} all-to-all(f32[1216,2,128]{2,1,0:T(2,128)S(1)} %bitcast.66), channel_id=1, replica_groups=mesh['grid'=32,'band_0'=2,'band_1'=2] {'grid','band_0'}, dimensions={0} | all-to-all | bytes 2490368 | tf_op jit(solution)/shard_map/all_to_all | solution.py:445
  241.1 3.6 %collective-permute-start.15 = (f32[4,4,4,16,128]{4,3,2,1,0:T(8,128)S(1)}, f32[4,4,4,16,128]{4,3,2,1,0:T(8,128)S(1)}, u32[]{:S(2)}, u32[]{:S(2)}) collective-permute-start(f32[4,4,4,16,128]{4,3,2,1,0:T(8,128)S(1)} %get-tuple-element.35.refs_6_), channel_id=1, source_target_pairs={{0,126},{1,127},{2,124},{3,125},{4,0},{5,1},{6,2},{7,3},{8,4},{9,5... | collective-permute-start | bytes 1572872 | tf_op jit(solution)/shard_map/ppermute | solution.py:434
  244.7 16.4 %shard_map.63 = (f32[512,512]{1,0:T(8,128)S(1)}, f32[8,128]{1,0:T(8,128)S(1)}) custom-call(s32[3]{0:T(128)S(1)} %pad_add_fusion.core_ref.refs_0_, f32[2432,128]{1,0:T(8,128)S(1)} %bitcast.47, f32[2432,128]{1,0:T(8,128)S(1)} %collective-permute-done.13.other_ref.refs_4_), custom_call_target="tpu_custom_call" | custom-call | flops 20000000000 | bytes 2490368 | tf_op jit(solution)/shard_map/pallas_call | solution.py:476
  261.1 3.4 %collective-permute-done.14.refs_7_ = f32[4,4,4,16,128]{4,3,2,1,0:T(8,128)S(1)} collective-permute-done((f32[4,4,4,16,128]{4,3,2,1,0:T(8,128)S(1)}, f32[4,4,4,16,128]{4,3,2,1,0:T(8,128)S(1)}, u32[]{:S(2)}, u32[]{:S(2)}) %collective-permute-start.14) | collective-permute-done | bytes 524320 | tf_op jit(solution)/shard_map/ppermute | solution.py:433
  264.5 2.9 shard_map.64
  267.5 1.2 collective-permute-done.21
  269.4 6.4 %all-to-all-start.7 = ((f32[192,2,128]{2,1,0:T(2,128)}), f32[192,2,128]{2,1,0:T(2,128)S(1)}, u32[]{:S(2)}, u32[]{:S(2)}) async-start(f32[192,2,128]{2,1,0:T(2,128)} %bitcast.26), calls=%async_computation.7 | async-start | bytes 393216 | tf_op jit(solution)/shard_map/all_to_all | solution.py:445
  276.6 0.9 collective-permute-start.20
  278.4 7.5 %all-to-all-done.7 = f32[192,2,128]{2,1,0:T(2,128)S(1)} async-done(((f32[192,2,128]{2,1,0:T(2,128)}), f32[192,2,128]{2,1,0:T(2,128)S(1)}, u32[]{:S(2)}, u32[]{:S(2)}) %all-to-all-start.7) | async-done | bytes 196640 | tf_op jit(solution)/shard_map/all_to_all | solution.py:445
  286.1 4.9 %collective-permute-done.19.across_ref = f32[2,4,4,16,128]{4,3,2,1,0:T(8,128)S(1)} collective-permute-done((f32[2,4,4,16,128]{4,3,2,1,0:T(8,128)S(1)}, f32[2,4,4,16,128]{4,3,2,1,0:T(8,128)S(1)}, u32[]{:S(2)}, u32[]{:S(2)}) %collective-permute-start.19) | collective-permute-done | bytes 262176 | tf_op jit(solution)/shard_map/ppermute | solution.py:532
  291.1 1.5 shard_map.65
  (66 shorter events, 8.6 us)
Async XLA Ops:
  0.6 73.1 %copy-start = (f32[4,16,16]{2,1,0:T(8,128)S(1)}, f32[4,16,16]{2,1,0:T(8,128)}, u32[]{:S(2)}) copy-start(f32[4,16,16]{2,1,0:T(8,128)} %param.5) | copy-start | bytes 12292
  3.2 17.9 %all-to-all-start = ((f32[4,2,4,4,16,128]{5,4,3,2,1,0:T(8,128)}), f32[4,2,4,4,16,128]{5,4,3,2,1,0:T(8,128)S(1)}, u32[]{:S(2)}, u32[]{:S(2)}) async-start(f32[4,2,4,4,16,128]{5,4,3,2,1,0:T(8,128)} %bitcast.6), calls=%async_computation | async-start | bytes 2097152 | tf_op jit(solution)/shard_map/all_to_all | solution.py:470
  22.9 2.5 collective-permute-start
  73.7 4.0 %collective-permute-start.1 = (f32[1664,128]{1,0:T(8,128)S(1)}, f32[1664,128]{1,0:T(8,128)S(1)}, u32[]{:S(2)}, u32[]{:S(2)}) collective-permute-start(f32[1664,128]{1,0:T(8,128)S(1)} %bitcast.52), channel_id=1, source_target_pairs={{0,1},{1,0},{2,3},{3,2},{4,5},{5,4},{6,7},{7,6},{8,9},{9,8},{10,11... | collective-permute-start | bytes 2555912 | tf_op jit(solution)/shard_map/ppermute | solution.py:441
  73.7 19.8 %collective-permute-start.5 = (f32[4,4,4,16,128]{4,3,2,1,0:T(8,128)S(1)}, f32[4,4,4,16,128]{4,3,2,1,0:T(8,128)S(1)}, u32[]{:S(2)}, u32[]{:S(2)}) collective-permute-start(f32[4,4,4,16,128]{4,3,2,1,0:T(8,128)S(1)} %get-tuple-element.45.v_ref), channel_id=1, source_target_pairs={{0,3},{1,0},{2,1},{3,2},{4,7},{5,4},{6,5},{7,6},{8,11},{9,8},{10,9... | collective-permute-start | bytes 1572872 | tf_op jit(solution)/shard_map/ppermute | solution.py:436
  74.5 19.1 %collective-permute-start.4 = (f32[4,4,4,16,128]{4,3,2,1,0:T(8,128)S(1)}, f32[4,4,4,16,128]{4,3,2,1,0:T(8,128)S(1)}, u32[]{:S(2)}, u32[]{:S(2)}) collective-permute-start(f32[4,4,4,16,128]{4,3,2,1,0:T(8,128)S(1)} %get-tuple-element.45.v_ref), channel_id=1, source_target_pairs={{0,1},{1,2},{2,3},{3,0},{4,5},{5,6},{6,7},{7,4},{8,9},{9,10},{10,1... | collective-permute-start | bytes 1572872 | tf_op jit(solution)/shard_map/ppermute | solution.py:435
  74.5 19.1 %collective-permute-start.3 = (f32[4,4,4,16,128]{4,3,2,1,0:T(8,128)S(1)}, f32[4,4,4,16,128]{4,3,2,1,0:T(8,128)S(1)}, u32[]{:S(2)}, u32[]{:S(2)}) collective-permute-start(f32[4,4,4,16,128]{4,3,2,1,0:T(8,128)S(1)} %get-tuple-element.45.v_ref), channel_id=1, source_target_pairs={{0,126},{1,127},{2,124},{3,125},{4,0},{5,1},{6,2},{7,3},{8,4},{9,5... | collective-permute-start | bytes 1572872 | tf_op jit(solution)/shard_map/ppermute | solution.py:434
  77.8 19.8 %collective-permute-start.2 = (f32[4,4,4,16,128]{4,3,2,1,0:T(8,128)S(1)}, f32[4,4,4,16,128]{4,3,2,1,0:T(8,128)S(1)}, u32[]{:S(2)}, u32[]{:S(2)}) collective-permute-start(f32[4,4,4,16,128]{4,3,2,1,0:T(8,128)S(1)} %get-tuple-element.45.v_ref), channel_id=1, source_target_pairs={{0,4},{1,5},{2,6},{3,7},{4,8},{5,9},{6,10},{7,11},{8,12},{9,13},{1... | collective-permute-start | bytes 1572872 | tf_op jit(solution)/shard_map/ppermute | solution.py:433
  102.1 3.2 %copy-start.1 = (f32[4,4,4,16,128]{4,3,2,1,0:T(8,128)}, f32[4,4,4,16,128]{4,3,2,1,0:T(8,128)S(1)}, u32[]{:S(2)}) copy-start(f32[4,4,4,16,128]{4,3,2,1,0:T(8,128)S(1)} %get-tuple-element.29.v_ref) | copy-start | bytes 1572868
  102.1 3.2 %copy-start.3 = (f32[4,256,128]{2,1,0:T(8,128)}, f32[4,256,128]{2,1,0:T(8,128)S(1)}, u32[]{:S(2)}) copy-start(f32[4,256,128]{2,1,0:T(8,128)S(1)} %get-tuple-element.28.old_ref) | copy-start | bytes 1572868
  102.1 3.0 %collective-permute-start.6 = (f32[2432,128]{1,0:T(8,128)S(1)}, f32[2432,128]{1,0:T(8,128)S(1)}, u32[]{:S(2)}, u32[]{:S(2)}) collective-permute-start(f32[2432,128]{1,0:T(8,128)S(1)} %get-tuple-element.25), channel_id=1, source_target_pairs={{0,1},{1,0},{2,3},{3,2},{4,5},{5,4},{6,7},{7,6},{8,9},{9,8},{10,11... | collective-permute-start | bytes 3735560 | tf_op jit(solution)/shard_map/ppermute | solution.py:441
  131.6 25.2 %copy-start.2 = (f32[4,4,4,16,128]{4,3,2,1,0:T(8,128)S(1)}, f32[4,4,4,16,128]{4,3,2,1,0:T(8,128)}, u32[]{:S(2)}) copy-start(f32[4,4,4,16,128]{4,3,2,1,0:T(8,128)} %copy-done.1) | copy-start | bytes 1572868
  156.8 4.3 %collective-permute-start.7 = (f32[2432,128]{1,0:T(8,128)S(1)}, f32[2432,128]{1,0:T(8,128)S(1)}, u32[]{:S(2)}, u32[]{:S(2)}) collective-permute-start(f32[2432,128]{1,0:T(8,128)S(1)} %bitcast.49), channel_id=1, source_target_pairs={{0,1},{1,0},{2,3},{3,2},{4,5},{5,4},{6,7},{7,6},{8,9},{9,8},{10,11... | collective-permute-start | bytes 3735560 | tf_op jit(solution)/shard_map/ppermute | solution.py:441
  156.8 24.1 %copy-start.4 = (f32[4,256,128]{2,1,0:T(8,128)S(1)}, f32[4,256,128]{2,1,0:T(8,128)}, u32[]{:S(2)}) copy-start(f32[4,256,128]{2,1,0:T(8,128)} %copy-done.3) | copy-start | bytes 1572868
  156.8 20.7 %collective-permute-start.11 = (f32[4,4,4,16,128]{4,3,2,1,0:T(8,128)S(1)}, f32[4,4,4,16,128]{4,3,2,1,0:T(8,128)S(1)}, u32[]{:S(2)}, u32[]{:S(2)}) collective-permute-start(f32[4,4,4,16,128]{4,3,2,1,0:T(8,128)S(1)} %copy-done.2), channel_id=1, source_target_pairs={{0,3},{1,0},{2,1},{3,2},{4,7},{5,4},{6,5},{7,6},{8,11},{9,8},{10,9... | collective-permute-start | bytes 1572872 | tf_op jit(solution)/shard_map/ppermute | solution.py:436
  157.4 20.0 %collective-permute-start.10 = (f32[4,4,4,16,128]{4,3,2,1,0:T(8,128)S(1)}, f32[4,4,4,16,128]{4,3,2,1,0:T(8,128)S(1)}, u32[]{:S(2)}, u32[]{:S(2)}) collective-permute-start(f32[4,4,4,16,128]{4,3,2,1,0:T(8,128)S(1)} %copy-done.2), channel_id=1, source_target_pairs={{0,1},{1,2},{2,3},{3,0},{4,5},{5,6},{6,7},{7,4},{8,9},{9,10},{10,1... | collective-permute-start | bytes 1572872 | tf_op jit(solution)/shard_map/ppermute | solution.py:435
  157.4 20.0 %collective-permute-start.9 = (f32[4,4,4,16,128]{4,3,2,1,0:T(8,128)S(1)}, f32[4,4,4,16,128]{4,3,2,1,0:T(8,128)S(1)}, u32[]{:S(2)}, u32[]{:S(2)}) collective-permute-start(f32[4,4,4,16,128]{4,3,2,1,0:T(8,128)S(1)} %copy-done.2), channel_id=1, source_target_pairs={{0,126},{1,127},{2,124},{3,125},{4,0},{5,1},{6,2},{7,3},{8,4},{9,5... | collective-permute-start | bytes 1572872 | tf_op jit(solution)/shard_map/ppermute | solution.py:434
  161.0 19.8 %collective-permute-start.8 = (f32[4,4,4,16,128]{4,3,2,1,0:T(8,128)S(1)}, f32[4,4,4,16,128]{4,3,2,1,0:T(8,128)S(1)}, u32[]{:S(2)}, u32[]{:S(2)}) collective-permute-start(f32[4,4,4,16,128]{4,3,2,1,0:T(8,128)S(1)} %copy-done.2), channel_id=1, source_target_pairs={{0,4},{1,5},{2,6},{3,7},{4,8},{5,9},{6,10},{7,11},{8,12},{9,13},{1... | collective-permute-start | bytes 1572872 | tf_op jit(solution)/shard_map/ppermute | solution.py:433
  185.3 3.0 %collective-permute-start.12 = (f32[2432,128]{1,0:T(8,128)S(1)}, f32[2432,128]{1,0:T(8,128)S(1)}, u32[]{:S(2)}, u32[]{:S(2)}) collective-permute-start(f32[2432,128]{1,0:T(8,128)S(1)} %get-tuple-element.31), channel_id=1, source_target_pairs={{0,1},{1,0},{2,3},{3,2},{4,5},{5,4},{6,7},{7,6},{8,9},{9,8},{10,11... | collective-permute-start | bytes 3735560 | tf_op jit(solution)/shard_map/ppermute | solution.py:441
  240.4 4.3 %collective-permute-start.13 = (f32[2432,128]{1,0:T(8,128)S(1)}, f32[2432,128]{1,0:T(8,128)S(1)}, u32[]{:S(2)}, u32[]{:S(2)}) collective-permute-start(f32[2432,128]{1,0:T(8,128)S(1)} %bitcast.46), channel_id=1, source_target_pairs={{0,1},{1,0},{2,3},{3,2},{4,5},{5,4},{6,7},{7,6},{8,9},{9,8},{10,11... | collective-permute-start | bytes 3735560 | tf_op jit(solution)/shard_map/ppermute | solution.py:441
  240.4 20.6 %collective-permute-start.17 = (f32[4,4,4,16,128]{4,3,2,1,0:T(8,128)S(1)}, f32[4,4,4,16,128]{4,3,2,1,0:T(8,128)S(1)}, u32[]{:S(2)}, u32[]{:S(2)}) collective-permute-start(f32[4,4,4,16,128]{4,3,2,1,0:T(8,128)S(1)} %get-tuple-element.35.refs_6_), channel_id=1, source_target_pairs={{0,3},{1,0},{2,1},{3,2},{4,7},{5,4},{6,5},{7,6},{8,11},{9,8},{10,9... | collective-permute-start | bytes 1572872 | tf_op jit(solution)/shard_map/ppermute | solution.py:436
  241.1 20.0 %collective-permute-start.16 = (f32[4,4,4,16,128]{4,3,2,1,0:T(8,128)S(1)}, f32[4,4,4,16,128]{4,3,2,1,0:T(8,128)S(1)}, u32[]{:S(2)}, u32[]{:S(2)}) collective-permute-start(f32[4,4,4,16,128]{4,3,2,1,0:T(8,128)S(1)} %get-tuple-element.35.refs_6_), channel_id=1, source_target_pairs={{0,1},{1,2},{2,3},{3,0},{4,5},{5,6},{6,7},{7,4},{8,9},{9,10},{10,1... | collective-permute-start | bytes 1572872 | tf_op jit(solution)/shard_map/ppermute | solution.py:435
  241.1 20.0 %collective-permute-start.15 = (f32[4,4,4,16,128]{4,3,2,1,0:T(8,128)S(1)}, f32[4,4,4,16,128]{4,3,2,1,0:T(8,128)S(1)}, u32[]{:S(2)}, u32[]{:S(2)}) collective-permute-start(f32[4,4,4,16,128]{4,3,2,1,0:T(8,128)S(1)} %get-tuple-element.35.refs_6_), channel_id=1, source_target_pairs={{0,126},{1,127},{2,124},{3,125},{4,0},{5,1},{6,2},{7,3},{8,4},{9,5... | collective-permute-start | bytes 1572872 | tf_op jit(solution)/shard_map/ppermute | solution.py:434
  244.7 19.8 %collective-permute-start.14 = (f32[4,4,4,16,128]{4,3,2,1,0:T(8,128)S(1)}, f32[4,4,4,16,128]{4,3,2,1,0:T(8,128)S(1)}, u32[]{:S(2)}, u32[]{:S(2)}) collective-permute-start(f32[4,4,4,16,128]{4,3,2,1,0:T(8,128)S(1)} %get-tuple-element.35.refs_6_), channel_id=1, source_target_pairs={{0,4},{1,5},{2,6},{3,7},{4,8},{5,9},{6,10},{7,11},{8,12},{9,13},{1... | collective-permute-start | bytes 1572872 | tf_op jit(solution)/shard_map/ppermute | solution.py:433
  267.4 1.2 collective-permute-start.21
  269.4 16.5 %all-to-all-start.7 = ((f32[192,2,128]{2,1,0:T(2,128)}), f32[192,2,128]{2,1,0:T(2,128)S(1)}, u32[]{:S(2)}, u32[]{:S(2)}) async-start(f32[192,2,128]{2,1,0:T(2,128)} %bitcast.26), calls=%async_computation.7 | async-start | bytes 393216 | tf_op jit(solution)/shard_map/all_to_all | solution.py:445
  276.6 9.6 %collective-permute-start.20 = (f32[2,4,4,16,128]{4,3,2,1,0:T(8,128)}, f32[2,4,4,16,128]{4,3,2,1,0:T(8,128)S(1)}, u32[]{:S(2)}, u32[]{:S(2)}) collective-permute-start(f32[2,4,4,16,128]{4,3,2,1,0:T(8,128)} %get-tuple-element.41), channel_id=1, source_target_pairs={{0,3},{1,0},{2,1},{3,2},{4,7},{5,4},{6,5},{7,6},{8,11},{9,8},{10,9... | collective-permute-start | bytes 786440 | tf_op jit(solution)/shard_map/ppermute | solution.py:532
  277.4 13.6 %collective-permute-start.19 = (f32[2,4,4,16,128]{4,3,2,1,0:T(8,128)S(1)}, f32[2,4,4,16,128]{4,3,2,1,0:T(8,128)S(1)}, u32[]{:S(2)}, u32[]{:S(2)}) collective-permute-start(f32[2,4,4,16,128]{4,3,2,1,0:T(8,128)S(1)} %get-tuple-element.42), channel_id=1, source_target_pairs={{0,2},{1,3},{2,0},{3,1},{4,6},{5,7},{6,4},{7,5},{8,10},{9,11},{10,... | collective-permute-start | bytes 786440 | tf_op jit(solution)/shard_map/ppermute | solution.py:532
  278.2 12.9 %collective-permute-start.18 = (f32[2,4,4,16,128]{4,3,2,1,0:T(8,128)S(1)}, f32[2,4,4,16,128]{4,3,2,1,0:T(8,128)S(1)}, u32[]{:S(2)}, u32[]{:S(2)}) collective-permute-start(f32[2,4,4,16,128]{4,3,2,1,0:T(8,128)S(1)} %get-tuple-element.43), channel_id=1, source_target_pairs={{0,1},{1,2},{2,3},{3,0},{4,5},{5,6},{6,7},{7,4},{8,9},{9,10},{10,1... | collective-permute-start | bytes 786440 | tf_op jit(solution)/shard_map/ppermute | solution.py:532
  286.0 5.0 %collective-permute-start.22 = (f32[64,6,128]{2,1,0:T(8,128)S(1)}, f32[64,6,128]{2,1,0:T(8,128)S(1)}, u32[]{:S(2)}, u32[]{:S(2)}) collective-permute-start(f32[64,6,128]{2,1,0:T(8,128)S(1)} %reshape.78.here_ref), channel_id=1, source_target_pairs={{0,1},{1,0},{2,3},{3,2},{4,5},{5,4},{6,7},{7,6},{8,9},{9,8},{10,11... | collective-permute-start | bytes 589832 | tf_op jit(solution)/shard_map/ppermute | solution.py:441
where the time goes:
time: 294 us; the launch traced here: 293 us
  blocking collectives  150 us (51%)
  Pallas kernels  63.5 us (22%)
  waiting for transfers between devices  46.9 us (16%)
  starting transfers between devices  24.7 us (8%)
  other arithmetic  4 us (1%)
  local copies, waits for them, and re-layouts  3.51 us (1%)
    all_to_all x6, blocking collectives, exchange(): lax.all_to_all(pieces, CHIPS, split_axis=0, concat_axis=0, tiled=True)  150 us
    pallas_call x8, Pallas kernels, call(): pl.pallas_call(kernel, out_shape=[jax.ShapeDtypeStruct(s, jnp.float32) fo...  63.5 us
    all_to_all x1, waiting for transfers between devices, to_cells(): lax.all_to_all(jnp.moveaxis(pieces, 2, 0), BAND, split_axis=0, concat_axi...  14.3 us
    ppermute x3, waiting for transfers between devices, neighbours(): lax.ppermute(v, EVERY, slab_ring(1))  10.7 us
    ppermute x3, starting transfers between devices, neighbours(): lax.ppermute(v, EVERY, slab_ring(-1))  10.4 us
    ppermute x8, waiting for transfers between devices, swapped(): return lax.ppermute(x, 'band_1', ring(lax.axis_size('band_1'), 1))  9.39 us
    all_to_all x1, waiting for transfers between devices, exchange(): lax.all_to_all(pieces, CHIPS, split_axis=0, concat_axis=0, tiled=True)  7.53 us
    all_to_all x1, starting transfers between devices, exchange(): lax.all_to_all(pieces, CHIPS, split_axis=0, concat_axis=0, tiled=True)  6.37 us
  transfers between devices with their start and end apart: 25, of which 10 were waited for; matrix products, arithmetic and copies ran while one was open for 0% of the time, Pallas kernels for 17%

commit v1 on v0

--- a/solution.py
+++ b/solution.py
@@ -180,40 +180,46 @@
     return STEP_LENGTH / jnp.sqrt(squared + NORM_EPS)
 
 
+def apart_of(blocks):
+    return [(i, j) for i in range(blocks) for j in range(i + 1, blocks)]
+
+
 def factor_kernel(core_ref, mine_ref, other_ref, x_ref, stats_ref):
     blocks = x_ref.shape[0] // BLOCK
-    pairs = pairs_of(blocks)
-    spot = lax.broadcasted_iota(jnp.int32, (BLOCK, BLOCK), 0) == lax.broadcasted_iota(
-        jnp.int32, (BLOCK, BLOCK), 1
-    )
+    apart = apart_of(blocks)
+    row = lax.broadcasted_iota(jnp.int32, (BLOCK, BLOCK), 0)
+    lane = lax.broadcasted_iota(jnp.int32, (BLOCK, BLOCK), 1)
 
     def block(at):
         return block_of(core_ref[0], mine_ref, other_ref, at)
 
-    weights = block(2 * len(pairs) + blocks * blocks)[:TILE]
-    parts = {0: [], 1: []}
+    def upright(line):
+        return jnp.sum(jnp.where(row == lane, line, 0.0), axis=1, keepdims=True)
+
+    lines = block(2 * len(apart) + blocks)[: 3 * blocks]
+    rayleigh, energy, weight = (lines[blocks * k : blocks * (k + 1)] for k in range(3))
+    squared = squared_of(rayleigh, energy, weight)
+    stats_ref[:blocks, :] = rayleigh
+    stats_ref[blocks:, :] = squared
+    length = length_of(squared)
+    gain = 1.0 + rayleigh * length
+    diagonal = (length * energy - 2.0 * gain * rayleigh) * length + gain * gain * weight
+    d = [length[b : b + 1] for b in range(blocks)]
+    a = [gain[b : b + 1] for b in range(blocks)]
+    d_up = [upright(line) for line in d]
+    a_up = [upright(line) for line in a]
+    for at, (i, j) in enumerate(apart):
+        x_ref[BLOCK * i : BLOCK * (i + 1), BLOCK * j : BLOCK * (j + 1)] = (
+            d_up[i] * d[j]
+        ) * block(len(apart) + at) - (a_up[i] * d[j] + d_up[i] * a[j]) * block(at)
     for b in range(blocks):
-        at = pairs.index((b, b))
-        products, energies = block(at), block(len(pairs) + at)
-        weight = jnp.broadcast_to(weights[b : b + 1], (BLOCK, BLOCK))
-        for axis in (0, 1):
-            rayleigh, energy, share = (
-                jnp.sum(jnp.where(spot, m, 0.0), axis=axis, keepdims=True)
-                for m in (products, energies, weight)
-            )
-            squared = squared_of(rayleigh, energy, share)
-            length = length_of(squared)
-            parts[axis].append((1.0 + rayleigh * length, length, share))
-            if axis == 0:
-                stats_ref[b : b + 1, :] = rayleigh
-                stats_ref[blocks + b : blocks + b + 1, :] = squared
-    for at, (i, j) in enumerate(pairs):
-        a_i, d_i, _ = parts[1][i]
-        a_j, d_j, share = parts[0][j]
-        value = (d_i * d_j) * block(len(pairs) + at) - (a_i * d_j + d_i * a_j) * block(at)
-        if i == j:
-            value = value + jnp.where(spot, a_j * a_j * share, 0.0)
-        x_ref[BLOCK * i : BLOCK * (i + 1), BLOCK * j : BLOCK * (j + 1)] = value
+        both = block(2 * len(apart) + b)
+        energies = jnp.transpose(jnp.where(row > lane, both, 0.0))
+        upper = (d_up[b] * d[b]) * energies - (a_up[b] * d[b] + d_up[b] * a[b]) * both
+        upper = jnp.where(row < lane, upper, 0.0)
+        x_ref[BLOCK * b : BLOCK * (b + 1), BLOCK * b : BLOCK * (b + 1)] = (
+            upper + jnp.transpose(upper) + jnp.where(row == lane, diagonal[b : b + 1], 0.0)
+        )
     factorize(x_ref)
 
 
@@ -352,11 +358,29 @@
     for b in range(blocks):
         vp_ref[b] = cut(vp, b)
         w_ref[b] = cut(w, b).reshape(w_ref.shape[1:])
-    at = write_pairs(vp, w, 0, packed_ref)
-    at = write_pairs(w, w, at, packed_ref)
-    at = write_coupling(xi, w, at, packed_ref)
-    packed_ref[BLOCK * at :, :] = jnp.zeros((packed_ref.shape[0] - BLOCK * at, BLOCK), jnp.float32)
-    packed_ref[BLOCK * at : BLOCK * at + blocks, :] = jnp.concatenate(line_sums(vp * vp), axis=0)
+    row = lax.broadcasted_iota(jnp.int32, (BLOCK, BLOCK), 0)
+    lane = lax.broadcasted_iota(jnp.int32, (BLOCK, BLOCK), 1)
+    count = blocks * (blocks - 1) // 2
+    at = 0
+
+    def put(at, value):
+        packed_ref[BLOCK * at : BLOCK * (at + 1), :] = value
+
+    for i in range(blocks):
+        right = w[:, BLOCK * i :]
+        products = dot(cut(vp, i), right, (0, 0))
+        energies = dot(cut(w, i), right, (0, 0))
+        put(2 * count + i, jnp.where(row <= lane, cut(products, 0), cut(energies, 0)))
+        for j in range(1, blocks - i):
+            put(at, cut(products, j))
+            put(count + at, cut(energies, j))
+            at += 1
+    at = 2 * count + blocks
+    put(at, jnp.zeros((BLOCK, BLOCK), jnp.float32))
+    lines = line_sums(vp * w) + line_sums(w * w) + line_sums(vp * vp)
+    packed_ref[BLOCK * at : BLOCK * at + len(lines), :] = jnp.concatenate(lines, axis=0)
+    at = write_coupling(xi, w, at + 1, packed_ref)
+    put(at, jnp.zeros((BLOCK, BLOCK), jnp.float32))
     share_out(core, packed_ref, mine_ref, other_ref)
 
 
@@ -394,7 +418,7 @@
     right_ref, p_ref, xi_ref, vp_ref, w_ref, mine_ref, other_ref, c_ref, u_ref, packed_ref,
 ):
     blocks = v_ref.shape[0]
-    at = 2 * len(pairs_of(blocks))
+    at = 2 * len(apart_of(blocks)) + blocks + 1
     fill_coupling(c_ref, core_ref[0], in_mine_ref, in_other_ref, at)
     local_part(v_ref, (below_ref, above_ref, left_ref, right_ref), p_ref, u_ref)
     xi = joined(xi_ref)
@@ -503,7 +527,7 @@
         return (BLOCK * count, BLOCK), (BLOCK * count // 2, BLOCK)
 
     small, small_half = packed(pairs + blocks * blocks)
-    large, large_half = packed(2 * pairs + blocks * blocks + 2)
+    large, large_half = packed(blocks * (blocks - 1) + blocks + 2 + blocks * blocks)
     sums = (3 * blocks // 2, BLOCK)
     stats_shape = (2 * blocks, BLOCK)
     stats_list = []

time: 294 us -> 287 us (0.976)
  blocking collectives: 150 us -> 144 us
    all_to_all x6, blocking collectives: 150 us -> 144 us  [exchange(): lax.all_to_all(pieces, CHIPS, split_axis=0, concat_axis=0, tiled=True)]
where the time goes in v1:
time: 287 us; the launch traced here: 286 us
  blocking collectives  144 us (50%)
  Pallas kernels  63.3 us (22%)
  waiting for transfers between devices  46.6 us (16%)
  starting transfers between devices  24.4 us (9%)
  other arithmetic  3.85 us (1%)
  local copies, waits for them, and re-layouts  3.44 us (1%)
    all_to_all x6, blocking collectives, exchange(): lax.all_to_all(pieces, CHIPS, split_axis=0, concat_axis=0, tiled=True)  144 us
    pallas_call x8, Pallas kernels, call(): pl.pallas_call(kernel, out_shape=[jax.ShapeDtypeStruct(s, jnp.float32) fo...  63.3 us
    all_to_all x1, waiting for transfers between devices, to_cells(): lax.all_to_all(jnp.moveaxis(pieces, 2, 0), BAND, split_axis=0, concat_axi...  14.3 us
    ppermute x3, waiting for transfers between devices, neighbours(): lax.ppermute(v, EVERY, slab_ring(1))  10.8 us
    ppermute x3, starting transfers between devices, neighbours(): lax.ppermute(v, EVERY, slab_ring(-1))  10.2 us
    ppermute x8, waiting for transfers between devices, swapped(): return lax.ppermute(x, 'band_1', ring(lax.axis_size('band_1'), 1))  9.01 us
    all_to_all x1, waiting for transfers between devices, exchange(): lax.all_to_all(pieces, CHIPS, split_axis=0, concat_axis=0, tiled=True)  7.52 us
    all_to_all x1, starting transfers between devices, exchange(): lax.all_to_all(pieces, CHIPS, split_axis=0, concat_axis=0, tiled=True)  6.31 us
  transfers between devices with their start and end apart: 25, of which 10 were waited for; matrix products, arithmetic and copies ran while one was open for 0% of the time, Pallas kernels for 17%

profile of v1, /device:TPU:0, one launch (start us, length us, event | category | flops | bytes accessed | tf_op | source)
XLA Modules:
  0.0 286.3 jit_solution(5261487100629421663)
XLA Ops:
  0.7 1.3 pad_maximum_fusion
  2.1 1.1 reverse_select_fusion
  3.2 3.5 %all-to-all-start = ((f32[4,2,4,4,16,128]{5,4,3,2,1,0:T(8,128)}), f32[4,2,4,4,16,128]{5,4,3,2,1,0:T(8,128)S(1)}, u32[]{:S(2)}, u32[]{:S(2)}) async-start(f32[4,2,4,4,16,128]{5,4,3,2,1,0:T(8,128)} %bitcast.6), calls=%async_computation | async-start | bytes 2097152 | tf_op jit(solution)/shard_map/all_to_all | solution.py:494
  6.8 14.3 %all-to-all-done = f32[4,2,4,4,16,128]{5,4,3,2,1,0:T(8,128)S(1)} async-done(((f32[4,2,4,4,16,128]{5,4,3,2,1,0:T(8,128)}), f32[4,2,4,4,16,128]{5,4,3,2,1,0:T(8,128)S(1)}, u32[]{:S(2)}, u32[]{:S(2)}) %all-to-all-start) | async-done | bytes 1048608 | tf_op jit(solution)/shard_map/all_to_all | solution.py:494
  21.3 1.6 shard_map.58
  22.9 2.4 collective-permute-done
  25.4 27.6 %all_to_all.40 = f32[832,2,128]{2,1,0:T(2,128)S(1)} all-to-all(f32[832,2,128]{2,1,0:T(2,128)S(1)} %bitcast.69), channel_id=1, replica_groups=mesh['grid'=32,'band_0'=2,'band_1'=2] {'grid','band_0'}, dimensions={0} | all-to-all | bytes 1703936 | tf_op jit(solution)/shard_map/all_to_all | solution.py:469
  53.5 20.2 %all_to_all.41 = f32[832,2,128]{2,1,0:T(2,128)S(1)} all-to-all(f32[832,2,128]{2,1,0:T(2,128)S(1)} %bitcast.71), channel_id=1, replica_groups=mesh['grid'=32,'band_0'=2,'band_1'=2] {'grid','band_0'}, dimensions={0} | all-to-all | bytes 1703936 | tf_op jit(solution)/shard_map/all_to_all | solution.py:469
  74.5 3.3 %collective-permute-start.3 = (f32[4,4,4,16,128]{4,3,2,1,0:T(8,128)S(1)}, f32[4,4,4,16,128]{4,3,2,1,0:T(8,128)S(1)}, u32[]{:S(2)}, u32[]{:S(2)}) collective-permute-start(f32[4,4,4,16,128]{4,3,2,1,0:T(8,128)S(1)} %get-tuple-element.45.v_ref), channel_id=1, source_target_pairs={{0,126},{1,127},{2,124},{3,125},{4,0},{5,1},{6,2},{7,3},{8,4},{9,5... | collective-permute-start | bytes 1572872 | tf_op jit(solution)/shard_map/ppermute | solution.py:458
  77.8 15.8 %shard_map.59.x_ref = f32[512,512]{1,0:T(8,128)S(1)} custom-call(s32[3]{0:T(128)S(1)} %pad_add_fusion.core_ref.refs_0_, f32[1664,128]{1,0:T(8,128)S(1)} %bitcast.53, f32[1664,128]{1,0:T(8,128)S(1)} %collective-permute-done.1.other_ref.in_other_ref), custom_call_target="tpu_custom_call" | custom-call | flops 20000000000 | bytes 1703936 | tf_op jit(solution)/shard_map/pallas_call | solution.py:500
  93.6 3.9 %collective-permute-done.2.below_ref = f32[4,4,4,16,128]{4,3,2,1,0:T(8,128)S(1)} collective-permute-done((f32[4,4,4,16,128]{4,3,2,1,0:T(8,128)S(1)}, f32[4,4,4,16,128]{4,3,2,1,0:T(8,128)S(1)}, u32[]{:S(2)}, u32[]{:S(2)}) %collective-permute-start.2) | collective-permute-done | bytes 524320 | tf_op jit(solution)/shard_map/ppermute | solution.py:457
  97.6 4.4 %shard_map.60 = (f32[4,256,128]{2,1,0:T(8,128)S(1)}, f32[4,4,4,16,128]{4,3,2,1,0:T(8,128)S(1)}, f32[2176,128]{1,0:T(8,128)S(1)}, f32[2176,128]{1,0:T(8,128)S(1)}) custom-call(s32[3]{0:T(128)S(1)} %pad_add_fusion.core_ref.refs_0_, f32[512,512]{1,0:T(8,128)S(1)} %shard_map.59.x_ref, f32[1664,128]{1,0:T(8,128)S(1)} %bitcast.54, ...), custom_call_target="tpu_custom_call" | custom-call | flops 2000000000 | bytes 6029312 | tf_op jit(solution)/shard_map/pallas_call | solution.py:500
  102.2 2.7 collective-permute-done.6
  105.1 24.2 %all_to_all.42 = f32[1088,2,128]{2,1,0:T(2,128)S(1)} all-to-all(f32[1088,2,128]{2,1,0:T(2,128)S(1)} %bitcast.63), channel_id=1, replica_groups=mesh['grid'=32,'band_0'=2,'band_1'=2] {'grid','band_0'}, dimensions={0} | all-to-all | bytes 2228224 | tf_op jit(solution)/shard_map/all_to_all | solution.py:469
  130.0 23.5 %all_to_all.43 = f32[1088,2,128]{2,1,0:T(2,128)S(1)} all-to-all(f32[1088,2,128]{2,1,0:T(2,128)S(1)} %bitcast.67), channel_id=1, replica_groups=mesh['grid'=32,'band_0'=2,'band_1'=2] {'grid','band_0'}, dimensions={0} | all-to-all | bytes 2228224 | tf_op jit(solution)/shard_map/all_to_all | solution.py:469
  154.2 3.5 %collective-permute-start.9 = (f32[4,4,4,16,128]{4,3,2,1,0:T(8,128)S(1)}, f32[4,4,4,16,128]{4,3,2,1,0:T(8,128)S(1)}, u32[]{:S(2)}, u32[]{:S(2)}) collective-permute-start(f32[4,4,4,16,128]{4,3,2,1,0:T(8,128)S(1)} %copy-done.2), channel_id=1, source_target_pairs={{0,126},{1,127},{2,124},{3,125},{4,0},{5,1},{6,2},{7,3},{8,4},{9,5... | collective-permute-start | bytes 1572872 | tf_op jit(solution)/shard_map/ppermute | solution.py:458
  157.7 16.3 %shard_map.61 = (f32[512,512]{1,0:T(8,128)S(1)}, f32[8,128]{1,0:T(8,128)S(1)}) custom-call(s32[3]{0:T(128)S(1)} %pad_add_fusion.core_ref.refs_0_, f32[2176,128]{1,0:T(8,128)S(1)} %bitcast.50, f32[2176,128]{1,0:T(8,128)S(1)} %collective-permute-done.7.other_ref.in_other_ref), custom_call_target="tpu_custom_call" | custom-call | flops 20000000000 | bytes 2228224 | tf_op jit(solution)/shard_map/pallas_call | solution.py:500
  174.0 3.4 %collective-permute-done.8.below_ref = f32[4,4,4,16,128]{4,3,2,1,0:T(8,128)S(1)} collective-permute-done((f32[4,4,4,16,128]{4,3,2,1,0:T(8,128)S(1)}, f32[4,4,4,16,128]{4,3,2,1,0:T(8,128)S(1)}, u32[]{:S(2)}, u32[]{:S(2)}) %collective-permute-start.8) | collective-permute-done | bytes 524320 | tf_op jit(solution)/shard_map/ppermute | solution.py:457
  177.5 4.5 %shard_map.62 = (f32[4,256,128]{2,1,0:T(8,128)S(1)}, f32[4,4,4,16,128]{4,3,2,1,0:T(8,128)S(1)}, f32[2176,128]{1,0:T(8,128)S(1)}, f32[2176,128]{1,0:T(8,128)S(1)}) custom-call(s32[3]{0:T(128)S(1)} %pad_add_fusion.core_ref.refs_0_, f32[512,512]{1,0:T(8,128)S(1)} %get-tuple-element.26.x_ref, f32[8,128]{1,0:T(8,128)S(1)} %get-tuple-element.27.stats_ref, ...), custom_call_target="tpu_custom_call" | custom-call | flops 2000000000 | bytes 7081984 | tf_op jit(solution)/shard_map/pallas_call | solution.py:500
  182.1 2.7 collective-permute-done.12
  184.9 24.7 %all_to_all.44 = f32[1088,2,128]{2,1,0:T(2,128)S(1)} all-to-all(f32[1088,2,128]{2,1,0:T(2,128)S(1)} %bitcast.64), channel_id=1, replica_groups=mesh['grid'=32,'band_0'=2,'band_1'=2] {'grid','band_0'}, dimensions={0} | all-to-all | bytes 2228224 | tf_op jit(solution)/shard_map/all_to_all | solution.py:469
  210.3 23.4 %all_to_all.45 = f32[1088,2,128]{2,1,0:T(2,128)S(1)} all-to-all(f32[1088,2,128]{2,1,0:T(2,128)S(1)} %bitcast.68), channel_id=1, replica_groups=mesh['grid'=32,'band_0'=2,'band_1'=2] {'grid','band_0'}, dimensions={0} | all-to-all | bytes 2228224 | tf_op jit(solution)/shard_map/all_to_all | solution.py:469
  234.4 3.5 %collective-permute-start.15 = (f32[4,4,4,16,128]{4,3,2,1,0:T(8,128)S(1)}, f32[4,4,4,16,128]{4,3,2,1,0:T(8,128)S(1)}, u32[]{:S(2)}, u32[]{:S(2)}) collective-permute-start(f32[4,4,4,16,128]{4,3,2,1,0:T(8,128)S(1)} %get-tuple-element.35.refs_6_), channel_id=1, source_target_pairs={{0,126},{1,127},{2,124},{3,125},{4,0},{5,1},{6,2},{7,3},{8,4},{9,5... | collective-permute-start | bytes 1572872 | tf_op jit(solution)/shard_map/ppermute | solution.py:458
  237.9 16.3 %shard_map.63 = (f32[512,512]{1,0:T(8,128)S(1)}, f32[8,128]{1,0:T(8,128)S(1)}) custom-call(s32[3]{0:T(128)S(1)} %pad_add_fusion.core_ref.refs_0_, f32[2176,128]{1,0:T(8,128)S(1)} %bitcast.47, f32[2176,128]{1,0:T(8,128)S(1)} %collective-permute-done.13.other_ref.refs_4_), custom_call_target="tpu_custom_call" | custom-call | flops 20000000000 | bytes 2228224 | tf_op jit(solution)/shard_map/pallas_call | solution.py:500
  254.2 3.4 %collective-permute-done.14.refs_7_ = f32[4,4,4,16,128]{4,3,2,1,0:T(8,128)S(1)} collective-permute-done((f32[4,4,4,16,128]{4,3,2,1,0:T(8,128)S(1)}, f32[4,4,4,16,128]{4,3,2,1,0:T(8,128)S(1)}, u32[]{:S(2)}, u32[]{:S(2)}) %collective-permute-start.14) | collective-permute-done | bytes 524320 | tf_op jit(solution)/shard_map/ppermute | solution.py:457
  257.7 2.9 %shard_map.64 = (f32[4,2,4,4,16,128]{5,4,3,2,1,0:T(8,128)S(1)}, f32[6,128]{1,0:T(8,128)S(1)}, f32[6,128]{1,0:T(8,128)S(1)}) custom-call(s32[3]{0:T(128)S(1)} %pad_add_fusion.core_ref.refs_0_, f32[512,512]{1,0:T(8,128)S(1)} %get-tuple-element.32.refs_1_, f32[8,128]{1,0:T(8,128)S(1)} %get-tuple-element.33.refs_2_, f32[2176,128]{1,0:T(8,128)S(1)} %bitcast.48, ...), custom_call_target="tpu_custom_call" | custom-call | flops 2000000000 | bytes 7081984 | tf_op jit(solution)/shard_map/pallas_call | solution.py:500
  260.7 1.2 collective-permute-done.21
  262.6 6.3 %all-to-all-start.7 = ((f32[192,2,128]{2,1,0:T(2,128)}), f32[192,2,128]{2,1,0:T(2,128)S(1)}, u32[]{:S(2)}, u32[]{:S(2)}) async-start(f32[192,2,128]{2,1,0:T(2,128)} %bitcast.26), calls=%async_computation.7 | async-start | bytes 393216 | tf_op jit(solution)/shard_map/all_to_all | solution.py:469
  269.7 0.9 collective-permute-start.20
  271.5 7.5 %all-to-all-done.7 = f32[192,2,128]{2,1,0:T(2,128)S(1)} async-done(((f32[192,2,128]{2,1,0:T(2,128)}), f32[192,2,128]{2,1,0:T(2,128)S(1)}, u32[]{:S(2)}, u32[]{:S(2)}) %all-to-all-start.7) | async-done | bytes 196640 | tf_op jit(solution)/shard_map/all_to_all | solution.py:469
  279.3 4.9 %collective-permute-done.19.across_ref = f32[2,4,4,16,128]{4,3,2,1,0:T(8,128)S(1)} collective-permute-done((f32[2,4,4,16,128]{4,3,2,1,0:T(8,128)S(1)}, f32[2,4,4,16,128]{4,3,2,1,0:T(8,128)S(1)}, u32[]{:S(2)}, u32[]{:S(2)}) %collective-permute-start.19) | collective-permute-done | bytes 262176 | tf_op jit(solution)/shard_map/ppermute | solution.py:556
  284.2 1.5 shard_map.65
  (66 shorter events, 8.4 us)
Async XLA Ops:
  0.6 73.1 %copy-start = (f32[4,16,16]{2,1,0:T(8,128)S(1)}, f32[4,16,16]{2,1,0:T(8,128)}, u32[]{:S(2)}) copy-start(f32[4,16,16]{2,1,0:T(8,128)} %param.5) | copy-start | bytes 12292
  3.2 17.9 %all-to-all-start = ((f32[4,2,4,4,16,128]{5,4,3,2,1,0:T(8,128)}), f32[4,2,4,4,16,128]{5,4,3,2,1,0:T(8,128)S(1)}, u32[]{:S(2)}, u32[]{:S(2)}) async-start(f32[4,2,4,4,16,128]{5,4,3,2,1,0:T(8,128)} %bitcast.6), calls=%async_computation | async-start | bytes 2097152 | tf_op jit(solution)/shard_map/all_to_all | solution.py:494
  22.9 2.5 collective-permute-start
  73.7 4.0 %collective-permute-start.1 = (f32[1664,128]{1,0:T(8,128)S(1)}, f32[1664,128]{1,0:T(8,128)S(1)}, u32[]{:S(2)}, u32[]{:S(2)}) collective-permute-start(f32[1664,128]{1,0:T(8,128)S(1)} %bitcast.52), channel_id=1, source_target_pairs={{0,1},{1,0},{2,3},{3,2},{4,5},{5,4},{6,7},{7,6},{8,9},{9,8},{10,11... | collective-permute-start | bytes 2555912 | tf_op jit(solution)/shard_map/ppermute | solution.py:465
  73.7 19.8 %collective-permute-start.5 = (f32[4,4,4,16,128]{4,3,2,1,0:T(8,128)S(1)}, f32[4,4,4,16,128]{4,3,2,1,0:T(8,128)S(1)}, u32[]{:S(2)}, u32[]{:S(2)}) collective-permute-start(f32[4,4,4,16,128]{4,3,2,1,0:T(8,128)S(1)} %get-tuple-element.45.v_ref), channel_id=1, source_target_pairs={{0,3},{1,0},{2,1},{3,2},{4,7},{5,4},{6,5},{7,6},{8,11},{9,8},{10,9... | collective-permute-start | bytes 1572872 | tf_op jit(solution)/shard_map/ppermute | solution.py:460
  74.5 19.1 %collective-permute-start.4 = (f32[4,4,4,16,128]{4,3,2,1,0:T(8,128)S(1)}, f32[4,4,4,16,128]{4,3,2,1,0:T(8,128)S(1)}, u32[]{:S(2)}, u32[]{:S(2)}) collective-permute-start(f32[4,4,4,16,128]{4,3,2,1,0:T(8,128)S(1)} %get-tuple-element.45.v_ref), channel_id=1, source_target_pairs={{0,1},{1,2},{2,3},{3,0},{4,5},{5,6},{6,7},{7,4},{8,9},{9,10},{10,1... | collective-permute-start | bytes 1572872 | tf_op jit(solution)/shard_map/ppermute | solution.py:459
  74.5 19.1 %collective-permute-start.3 = (f32[4,4,4,16,128]{4,3,2,1,0:T(8,128)S(1)}, f32[4,4,4,16,128]{4,3,2,1,0:T(8,128)S(1)}, u32[]{:S(2)}, u32[]{:S(2)}) collective-permute-start(f32[4,4,4,16,128]{4,3,2,1,0:T(8,128)S(1)} %get-tuple-element.45.v_ref), channel_id=1, source_target_pairs={{0,126},{1,127},{2,124},{3,125},{4,0},{5,1},{6,2},{7,3},{8,4},{9,5... | collective-permute-start | bytes 1572872 | tf_op jit(solution)/shard_map/ppermute | solution.py:458
  77.8 19.8 %collective-permute-start.2 = (f32[4,4,4,16,128]{4,3,2,1,0:T(8,128)S(1)}, f32[4,4,4,16,128]{4,3,2,1,0:T(8,128)S(1)}, u32[]{:S(2)}, u32[]{:S(2)}) collective-permute-start(f32[4,4,4,16,128]{4,3,2,1,0:T(8,128)S(1)} %get-tuple-element.45.v_ref), channel_id=1, source_target_pairs={{0,4},{1,5},{2,6},{3,7},{4,8},{5,9},{6,10},{7,11},{8,12},{9,13},{1... | collective-permute-start | bytes 1572872 | tf_op jit(solution)/shard_map/ppermute | solution.py:457
  102.1 3.0 %copy-start.1 = (f32[4,4,4,16,128]{4,3,2,1,0:T(8,128)}, f32[4,4,4,16,128]{4,3,2,1,0:T(8,128)S(1)}, u32[]{:S(2)}) copy-start(f32[4,4,4,16,128]{4,3,2,1,0:T(8,128)S(1)} %get-tuple-element.29.v_ref) | copy-start | bytes 1572868
  102.1 3.0 %copy-start.3 = (f32[4,256,128]{2,1,0:T(8,128)}, f32[4,256,128]{2,1,0:T(8,128)S(1)}, u32[]{:S(2)}) copy-start(f32[4,256,128]{2,1,0:T(8,128)S(1)} %get-tuple-element.28.old_ref) | copy-start | bytes 1572868
  102.1 2.8 collective-permute-start.6
  129.9 23.6 %copy-start.2 = (f32[4,4,4,16,128]{4,3,2,1,0:T(8,128)S(1)}, f32[4,4,4,16,128]{4,3,2,1,0:T(8,128)}, u32[]{:S(2)}) copy-start(f32[4,4,4,16,128]{4,3,2,1,0:T(8,128)} %copy-done.1) | copy-start | bytes 1572868
  153.5 4.2 %collective-permute-start.7 = (f32[2176,128]{1,0:T(8,128)S(1)}, f32[2176,128]{1,0:T(8,128)S(1)}, u32[]{:S(2)}, u32[]{:S(2)}) collective-permute-start(f32[2176,128]{1,0:T(8,128)S(1)} %bitcast.49), channel_id=1, source_target_pairs={{0,1},{1,0},{2,3},{3,2},{4,5},{5,4},{6,7},{7,6},{8,9},{9,8},{10,11... | collective-permute-start | bytes 3342344 | tf_op jit(solution)/shard_map/ppermute | solution.py:465
  153.5 24.0 %copy-start.4 = (f32[4,256,128]{2,1,0:T(8,128)S(1)}, f32[4,256,128]{2,1,0:T(8,128)}, u32[]{:S(2)}) copy-start(f32[4,256,128]{2,1,0:T(8,128)} %copy-done.3) | copy-start | bytes 1572868
  153.5 20.5 %collective-permute-start.11 = (f32[4,4,4,16,128]{4,3,2,1,0:T(8,128)S(1)}, f32[4,4,4,16,128]{4,3,2,1,0:T(8,128)S(1)}, u32[]{:S(2)}, u32[]{:S(2)}) collective-permute-start(f32[4,4,4,16,128]{4,3,2,1,0:T(8,128)S(1)} %copy-done.2), channel_id=1, source_target_pairs={{0,3},{1,0},{2,1},{3,2},{4,7},{5,4},{6,5},{7,6},{8,11},{9,8},{10,9... | collective-permute-start | bytes 1572872 | tf_op jit(solution)/shard_map/ppermute | solution.py:460
  154.2 19.8 %collective-permute-start.10 = (f32[4,4,4,16,128]{4,3,2,1,0:T(8,128)S(1)}, f32[4,4,4,16,128]{4,3,2,1,0:T(8,128)S(1)}, u32[]{:S(2)}, u32[]{:S(2)}) collective-permute-start(f32[4,4,4,16,128]{4,3,2,1,0:T(8,128)S(1)} %copy-done.2), channel_id=1, source_target_pairs={{0,1},{1,2},{2,3},{3,0},{4,5},{5,6},{6,7},{7,4},{8,9},{9,10},{10,1... | collective-permute-start | bytes 1572872 | tf_op jit(solution)/shard_map/ppermute | solution.py:459
  154.2 19.8 %collective-permute-start.9 = (f32[4,4,4,16,128]{4,3,2,1,0:T(8,128)S(1)}, f32[4,4,4,16,128]{4,3,2,1,0:T(8,128)S(1)}, u32[]{:S(2)}, u32[]{:S(2)}) collective-permute-start(f32[4,4,4,16,128]{4,3,2,1,0:T(8,128)S(1)} %copy-done.2), channel_id=1, source_target_pairs={{0,126},{1,127},{2,124},{3,125},{4,0},{5,1},{6,2},{7,3},{8,4},{9,5... | collective-permute-start | bytes 1572872 | tf_op jit(solution)/shard_map/ppermute | solution.py:458
  157.7 19.8 %collective-permute-start.8 = (f32[4,4,4,16,128]{4,3,2,1,0:T(8,128)S(1)}, f32[4,4,4,16,128]{4,3,2,1,0:T(8,128)S(1)}, u32[]{:S(2)}, u32[]{:S(2)}) collective-permute-start(f32[4,4,4,16,128]{4,3,2,1,0:T(8,128)S(1)} %copy-done.2), channel_id=1, source_target_pairs={{0,4},{1,5},{2,6},{3,7},{4,8},{5,9},{6,10},{7,11},{8,12},{9,13},{1... | collective-permute-start | bytes 1572872 | tf_op jit(solution)/shard_map/ppermute | solution.py:457
  182.0 2.8 collective-permute-start.12
  233.7 4.2 %collective-permute-start.13 = (f32[2176,128]{1,0:T(8,128)S(1)}, f32[2176,128]{1,0:T(8,128)S(1)}, u32[]{:S(2)}, u32[]{:S(2)}) collective-permute-start(f32[2176,128]{1,0:T(8,128)S(1)} %bitcast.46), channel_id=1, source_target_pairs={{0,1},{1,0},{2,3},{3,2},{4,5},{5,4},{6,7},{7,6},{8,9},{9,8},{10,11... | collective-permute-start | bytes 3342344 | tf_op jit(solution)/shard_map/ppermute | solution.py:465
  233.7 20.5 %collective-permute-start.17 = (f32[4,4,4,16,128]{4,3,2,1,0:T(8,128)S(1)}, f32[4,4,4,16,128]{4,3,2,1,0:T(8,128)S(1)}, u32[]{:S(2)}, u32[]{:S(2)}) collective-permute-start(f32[4,4,4,16,128]{4,3,2,1,0:T(8,128)S(1)} %get-tuple-element.35.refs_6_), channel_id=1, source_target_pairs={{0,3},{1,0},{2,1},{3,2},{4,7},{5,4},{6,5},{7,6},{8,11},{9,8},{10,9... | collective-permute-start | bytes 1572872 | tf_op jit(solution)/shard_map/ppermute | solution.py:460
  234.4 19.8 %collective-permute-start.16 = (f32[4,4,4,16,128]{4,3,2,1,0:T(8,128)S(1)}, f32[4,4,4,16,128]{4,3,2,1,0:T(8,128)S(1)}, u32[]{:S(2)}, u32[]{:S(2)}) collective-permute-start(f32[4,4,4,16,128]{4,3,2,1,0:T(8,128)S(1)} %get-tuple-element.35.refs_6_), channel_id=1, source_target_pairs={{0,1},{1,2},{2,3},{3,0},{4,5},{5,6},{6,7},{7,4},{8,9},{9,10},{10,1... | collective-permute-start | bytes 1572872 | tf_op jit(solution)/shard_map/ppermute | solution.py:459
  234.4 19.8 %collective-permute-start.15 = (f32[4,4,4,16,128]{4,3,2,1,0:T(8,128)S(1)}, f32[4,4,4,16,128]{4,3,2,1,0:T(8,128)S(1)}, u32[]{:S(2)}, u32[]{:S(2)}) collective-permute-start(f32[4,4,4,16,128]{4,3,2,1,0:T(8,128)S(1)} %get-tuple-element.35.refs_6_), channel_id=1, source_target_pairs={{0,126},{1,127},{2,124},{3,125},{4,0},{5,1},{6,2},{7,3},{8,4},{9,5... | collective-permute-start | bytes 1572872 | tf_op jit(solution)/shard_map/ppermute | solution.py:458
  237.9 19.8 %collective-permute-start.14 = (f32[4,4,4,16,128]{4,3,2,1,0:T(8,128)S(1)}, f32[4,4,4,16,128]{4,3,2,1,0:T(8,128)S(1)}, u32[]{:S(2)}, u32[]{:S(2)}) collective-permute-start(f32[4,4,4,16,128]{4,3,2,1,0:T(8,128)S(1)} %get-tuple-element.35.refs_6_), channel_id=1, source_target_pairs={{0,4},{1,5},{2,6},{3,7},{4,8},{5,9},{6,10},{7,11},{8,12},{9,13},{1... | collective-permute-start | bytes 1572872 | tf_op jit(solution)/shard_map/ppermute | solution.py:457
  260.6 1.2 collective-permute-start.21
  262.6 16.5 %all-to-all-start.7 = ((f32[192,2,128]{2,1,0:T(2,128)}), f32[192,2,128]{2,1,0:T(2,128)S(1)}, u32[]{:S(2)}, u32[]{:S(2)}) async-start(f32[192,2,128]{2,1,0:T(2,128)} %bitcast.26), calls=%async_computation.7 | async-start | bytes 393216 | tf_op jit(solution)/shard_map/all_to_all | solution.py:469
  269.7 9.6 %collective-permute-start.20 = (f32[2,4,4,16,128]{4,3,2,1,0:T(8,128)}, f32[2,4,4,16,128]{4,3,2,1,0:T(8,128)S(1)}, u32[]{:S(2)}, u32[]{:S(2)}) collective-permute-start(f32[2,4,4,16,128]{4,3,2,1,0:T(8,128)} %get-tuple-element.41), channel_id=1, source_target_pairs={{0,3},{1,0},{2,1},{3,2},{4,7},{5,4},{6,5},{7,6},{8,11},{9,8},{10,9... | collective-permute-start | bytes 786440 | tf_op jit(solution)/shard_map/ppermute | solution.py:556
  270.6 13.6 %collective-permute-start.19 = (f32[2,4,4,16,128]{4,3,2,1,0:T(8,128)S(1)}, f32[2,4,4,16,128]{4,3,2,1,0:T(8,128)S(1)}, u32[]{:S(2)}, u32[]{:S(2)}) collective-permute-start(f32[2,4,4,16,128]{4,3,2,1,0:T(8,128)S(1)} %get-tuple-element.42), channel_id=1, source_target_pairs={{0,2},{1,3},{2,0},{3,1},{4,6},{5,7},{6,4},{7,5},{8,10},{9,11},{10,... | collective-permute-start | bytes 786440 | tf_op jit(solution)/shard_map/ppermute | solution.py:556
  271.3 12.9 %collective-permute-start.18 = (f32[2,4,4,16,128]{4,3,2,1,0:T(8,128)S(1)}, f32[2,4,4,16,128]{4,3,2,1,0:T(8,128)S(1)}, u32[]{:S(2)}, u32[]{:S(2)}) collective-permute-start(f32[2,4,4,16,128]{4,3,2,1,0:T(8,128)S(1)} %get-tuple-element.43), channel_id=1, source_target_pairs={{0,1},{1,2},{2,3},{3,0},{4,5},{5,6},{6,7},{7,4},{8,9},{9,10},{10,1... | collective-permute-start | bytes 786440 | tf_op jit(solution)/shard_map/ppermute | solution.py:556
  279.2 5.0 %collective-permute-start.22 = (f32[64,6,128]{2,1,0:T(8,128)S(1)}, f32[64,6,128]{2,1,0:T(8,128)S(1)}, u32[]{:S(2)}, u32[]{:S(2)}) collective-permute-start(f32[64,6,128]{2,1,0:T(8,128)S(1)} %reshape.78.here_ref), channel_id=1, source_target_pairs={{0,1},{1,0},{2,3},{3,2},{4,5},{5,4},{6,7},{7,6},{8,9},{9,8},{10,11... | collective-permute-start | bytes 589832 | tf_op jit(solution)/shard_map/ppermute | solution.py:465

commit v2 on v1

--- a/solution.py
+++ b/solution.py
@@ -26,8 +26,8 @@
     return high, (x - high.astype(jnp.float32)).astype(jnp.bfloat16)
 
 
-def dot(left, right, sides):
-    (lh, ll), (rh, rl) = split(left), split(right)
+def dot_parts(left, right, sides):
+    (lh, ll), (rh, rl) = left, right
 
     def once(a, b):
         return lax.dot_general(
@@ -35,6 +35,14 @@
         )
 
     return once(lh, rl) + once(ll, rh) + once(lh, rh)
+
+
+def dot(left, right, sides):
+    return dot_parts(split(left), split(right), sides)
+
+
+def lanes_of(parts, start, stop):
+    return tuple(part[:, start:stop] for part in parts)
 
 
 def row_of(tile, j):
@@ -115,10 +123,27 @@
     return jnp.where(here, mine, other)
 
 
+def spread(x_ref, own, at):
+    size = x_ref.shape[0]
+    start, stop = BLOCK * at, BLOCK * (at + 1)
+    here, below = slice(start, stop), slice(stop, size)
+    around = [x_ref[here, part] for part in (slice(0, start), slice(stop, size)) if part.stop > part.start]
+    sides = dot(own, jnp.concatenate(around, axis=1), (1, 0))
+    row = jnp.concatenate(
+        [part for part in (sides[:, :start], own, sides[:, start:]) if part.shape[1]], axis=1
+    )
+    x_ref[here, :] = row
+    if stop < size:
+        parts = split(row)
+        change = dot_parts(lanes_of(parts, stop, size), parts, (0, 0))
+        x_ref[below, here] = -change[:, here]
+        x_ref[below, below] = x_ref[below, below] - change[:, stop:]
+        if start:
+            x_ref[below, :start] = x_ref[below, :start] - change[:, :start]
+
+
 def factorize(x_ref):
     blocks = x_ref.shape[0] // BLOCK
-    for i in range(1, blocks):
-        x_ref[BLOCK * i : BLOCK * (i + 1), : BLOCK * i] = jnp.zeros((BLOCK, BLOCK * i), jnp.float32)
     block_row = lax.broadcasted_iota(jnp.int32, (BLOCK, BLOCK), 0)
     block_lane = lax.broadcasted_iota(jnp.int32, (BLOCK, BLOCK), 1)
 
@@ -145,16 +170,12 @@
 
         lax.fori_loop(0, 2, part, 0)
         own = jnp.where((block_row < HALF) & (block_lane >= HALF), 0.0, x_ref[here, here])
-        x_ref[here, here] = jnp.where(block_row == block_lane, 1.0, 0.0)
-        x_ref[here, :] = dot(own, x_ref[here, :], (1, 0))
-
-        def update(i, carry):
-            there = pl.ds(pl.multiple_of(i * BLOCK, BLOCK), BLOCK)
-            x_ref[there, here] = jnp.zeros((BLOCK, BLOCK), jnp.float32)
-            x_ref[there, :] = x_ref[there, :] - dot(x_ref[here, there], x_ref[here, :], (0, 0))
-            return carry
-
-        return lax.fori_loop(k + 1, blocks, update, carry)
+        for at in range(blocks):
+            @pl.when(k == at)
+            def _(at=at):
+                spread(x_ref, own, at)
+
+        return carry
 
     lax.fori_loop(0, blocks, step, 0)
     for i in range(blocks - 1):
@@ -244,8 +265,8 @@
 
 
 def write_coupling(xi, v, at, packed_ref):
-    blocks = v.shape[1] // BLOCK
-    c = dot(xi, v, (0, 0))
+    c = dot_parts(xi, v, (0, 0))
+    blocks = c.shape[1] // BLOCK
     for j in range(blocks):
         packed_ref[BLOCK * at : BLOCK * (at + blocks), :] = cut(c, j)
         at += blocks
@@ -255,7 +276,7 @@
 def gram_kernel(core_ref, v_ref, xi_ref, mine_ref, other_ref, packed_ref):
     v = joined(v_ref)
     at = write_pairs(v, v, 0, packed_ref)
-    write_coupling(joined(xi_ref), v, at, packed_ref)
+    write_coupling(split(joined(xi_ref)), split(v), at, packed_ref)
     share_out(core_ref[0], packed_ref, mine_ref, other_ref)
 
 
@@ -287,8 +308,19 @@
                 v_ref[z, first_row + x] = vp - (ref[1, z, x] - rayleigh * vp) * length
 
 
-def local_part(v_ref, around, p_ref, u_ref):
-    below_ref, above_ref, left_ref, right_ref = around
+def local_part(core_ref, v_ref, around, p_ref, u_ref):
+    far_ref, close_ref, left_ref, right_ref = around
+
+    @pl.when(core_ref[3] == 0)
+    def _():
+        apply_local(v_ref, far_ref, close_ref, left_ref, right_ref, p_ref, u_ref)
+
+    @pl.when(core_ref[3] != 0)
+    def _():
+        apply_local(v_ref, close_ref, far_ref, left_ref, right_ref, p_ref, u_ref)
+
+
+def apply_local(v_ref, below_ref, above_ref, left_ref, right_ref, p_ref, u_ref):
     blocks, planes, rows, columns, _ = v_ref.shape
     along_z = [(ref, z) for ref in (below_ref, v_ref, above_ref) for z in range(planes)]
     along_x = [(ref, x) for ref in (left_ref, v_ref, right_ref) for x in range(rows)]
@@ -331,8 +363,13 @@
 
 def transformed(v, x):
     middle = x.shape[0] // 2
+    parts = split(v)
     return jnp.concatenate(
-        [dot(v[:, :middle], x[:middle, :middle], (1, 1)), dot(v, x[middle:, :], (1, 1))], axis=1
+        [
+            dot_parts(lanes_of(parts, 0, middle), split(x[:middle, :middle]), (1, 1)),
+            dot_parts(parts, split(x[middle:, :]), (1, 1)),
+        ],
+        axis=1,
     )
 
 
@@ -366,32 +403,41 @@
     def put(at, value):
         packed_ref[BLOCK * at : BLOCK * (at + 1), :] = value
 
+    left, right = split(vp), split(w)
+    total, middle = w.shape[1], w.shape[1] // 2
     for i in range(blocks):
-        right = w[:, BLOCK * i :]
-        products = dot(cut(vp, i), right, (0, 0))
-        energies = dot(cut(w, i), right, (0, 0))
-        put(2 * count + i, jnp.where(row <= lane, cut(products, 0), cut(energies, 0)))
-        for j in range(1, blocks - i):
-            put(at, cut(products, j))
-            put(count + at, cut(energies, j))
-            at += 1
+        top = BLOCK * i // middle * middle
+        if BLOCK * i == top:
+            products, energies = (
+                dot_parts(lanes_of(p, top, top + middle), lanes_of(right, top, total), (0, 0))
+                for p in (left, right)
+            )
+        lines = slice(BLOCK * i - top, BLOCK * (i + 1) - top)
+        for j in range(i, blocks):
+            lanes = slice(BLOCK * j - top, BLOCK * (j + 1) - top)
+            if i == j:
+                put(2 * count + i, jnp.where(row <= lane, products[lines, lanes], energies[lines, lanes]))
+            else:
+                put(at, products[lines, lanes])
+                put(count + at, energies[lines, lanes])
+                at += 1
     at = 2 * count + blocks
     put(at, jnp.zeros((BLOCK, BLOCK), jnp.float32))
     lines = line_sums(vp * w) + line_sums(w * w) + line_sums(vp * vp)
     packed_ref[BLOCK * at : BLOCK * at + len(lines), :] = jnp.concatenate(lines, axis=0)
-    at = write_coupling(xi, w, at + 1, packed_ref)
+    at = write_coupling(split(xi), right, at + 1, packed_ref)
     put(at, jnp.zeros((BLOCK, BLOCK), jnp.float32))
     share_out(core, packed_ref, mine_ref, other_ref)
 
 
 def first_transform_kernel(
-    core_ref, x_ref, in_mine_ref, in_other_ref, v_ref, below_ref, above_ref, left_ref, right_ref, p_ref,
+    core_ref, x_ref, in_mine_ref, in_other_ref, v_ref, far_ref, close_ref, left_ref, right_ref, p_ref,
     xi_ref, vp_ref, w_ref, mine_ref, other_ref, c_ref, u_ref, packed_ref,
 ):
     blocks = v_ref.shape[0]
     at = len(pairs_of(blocks))
     fill_coupling(c_ref, core_ref[0], in_mine_ref, in_other_ref, at)
-    local_part(v_ref, (below_ref, above_ref, left_ref, right_ref), p_ref, u_ref)
+    local_part(core_ref, v_ref, (far_ref, close_ref, left_ref, right_ref), p_ref, u_ref)
     v = flat_lanes(v_ref)
     xi = joined(xi_ref)
     z = flat_lanes(u_ref) - dot(xi, c_ref[...], (1, 0))
@@ -414,13 +460,13 @@
 
 
 def transform_kernel(
-    core_ref, x_ref, stats_ref, in_mine_ref, in_other_ref, old_ref, v_ref, below_ref, above_ref, left_ref,
+    core_ref, x_ref, stats_ref, in_mine_ref, in_other_ref, old_ref, v_ref, far_ref, close_ref, left_ref,
     right_ref, p_ref, xi_ref, vp_ref, w_ref, mine_ref, other_ref, c_ref, u_ref, packed_ref,
 ):
     blocks = v_ref.shape[0]
     at = 2 * len(apart_of(blocks)) + blocks + 1
     fill_coupling(c_ref, core_ref[0], in_mine_ref, in_other_ref, at)
-    local_part(v_ref, (below_ref, above_ref, left_ref, right_ref), p_ref, u_ref)
+    local_part(core_ref, v_ref, (far_ref, close_ref, left_ref, right_ref), p_ref, u_ref)
     xi = joined(xi_ref)
     y = flat_lanes(u_ref) - dot(xi, c_ref[...], (1, 0))
     v, z = stepped(joined(old_ref), flat_lanes(v_ref), y, stats_ref[...], blocks)
@@ -440,11 +486,11 @@
     return far * (lax.axis_size(BAND) // 2)
 
 
-def slab_ring(by):
+def slab_pairs(start):
     slabs, quarters = lax.axis_size("grid"), lax.axis_size(BAND)
 
     def pair(g, b):
-        there = (g + by) % slabs
+        there = (g + (1 if g % 2 == start else -1)) % slabs
         crosses = g // (slabs // 2) != there // (slabs // 2)
         return g * quarters + b, there * quarters + (b + crosses * (quarters // 2)) % quarters
 
@@ -453,12 +499,9 @@
 
 def neighbours(v):
     near = lax.axis_size(BAND)
-    return (
-        lax.ppermute(v, EVERY, slab_ring(1)),
-        lax.ppermute(v, EVERY, slab_ring(-1)),
-        lax.ppermute(v, BAND, ring(near, 1)),
-        lax.ppermute(v, BAND, ring(near, -1)),
-    )
+    far = lax.ppermute(v, EVERY, slab_pairs(1))
+    close = lax.ppermute(v, EVERY, slab_pairs(0))
+    return far, close, lax.ppermute(v, BAND, ring(near, 1)), lax.ppermute(v, BAND, ring(near, -1))
 
 
 def swapped(x):
@@ -485,18 +528,28 @@
     return half, swapped(half)
 
 
-def to_cells(*fields):
-    count = lax.axis_size(BAND)
-    z, x, y, lanes = fields[0].shape
-    pieces = jnp.stack([f.reshape(z, 2, count // 2, x // count, y, lanes) for f in fields])
-    pieces = jnp.where(turn() == 0, pieces, pieces[:, :, ::-1])
-    pieces = pieces.reshape(len(fields), z, count, x // count, y, lanes)
-    pieces = lax.all_to_all(jnp.moveaxis(pieces, 2, 0), BAND, split_axis=0, concat_axis=0, tiled=True)
-    return [pieces[:, at] for at in range(len(fields))]
+def pieces_kernel(core_ref, first_ref, second_ref, out_ref):
+    quarters, _, planes, rows, _, _ = out_ref.shape
+    for q in range(quarters):
+        first_row = rows * lax.rem(core_ref[2] + q, quarters)
+        for k, ref in enumerate((first_ref, second_ref)):
+            for z in range(planes):
+                for x in range(rows):
+                    out_ref[q, k, z, x] = ref[z, first_row + x]
+
+
+def to_cells(first, second):
+    quarters = lax.axis_size(BAND)
+    z, x, y, lanes = first.shape
+    shape = (quarters, 2, z, x // quarters, y, lanes)
+    (pieces,) = call(pieces_kernel, [shape], first, second, flops=1_000_000)
+    pieces = lax.all_to_all(pieces, BAND, split_axis=0, concat_axis=0, tiled=True)
+    return pieces[:, 0], pieces[:, 1]
 
 
 def call(kernel, shapes, *args, scratch=(), flops=2_000_000_000, room=32):
-    place = jnp.stack([lax.axis_index("band_1"), lax.axis_index(BAND), turn()]).astype(jnp.int32)
+    place = [lax.axis_index("band_1"), lax.axis_index(BAND), turn(), lax.axis_index("grid") % 2]
+    place = jnp.stack(place).astype(jnp.int32)
     return pl.pallas_call(
         kernel,
         out_shape=[jax.ShapeDtypeStruct(s, jnp.float32) for s in shapes],

time: 287 us -> 279 us (0.972)
  waiting for transfers between devices: 46.6 us -> 26.2 us
  blocking collectives: 144 us -> 161 us
  starting transfers between devices: 24.4 us -> 21.5 us
    all_to_all x0 -> x1, blocking collectives: none -> 17.1 us  [to_cells(): lax.all_to_all(pieces, BAND, split_axis=0, concat_axis=0, tiled=True)]
    all_to_all x1 -> x0, waiting for transfers between devices: 14.3 us -> none  [to_cells(): lax.all_to_all(jnp.moveaxis(pieces, 2, 0), BAND, split_axis=0, concat_axi...]
    ppermute x6, waiting for transfers between devices: 10.8 us -> 5.28 us  [the longest x3 5.27 us: neighbours(): far = lax.ppermute(v, EVERY, slab_pairs(1))]
    all_to_all x1 -> x0, starting transfers between devices: 3.51 us -> none  [to_cells(): lax.all_to_all(jnp.moveaxis(pieces, 2, 0), BAND, split_axis=0, concat_axi...]
    pallas_call x8 -> x9, Pallas kernels: 63.3 us -> 61.9 us  [call(): pl.pallas_call(kernel, out_shape=[jax.ShapeDtypeStruct(s, jnp.float32) fo...]
  transfers between devices with their start and end apart: 25 -> 24, of which waited for: 10 -> 9; matrix products, arithmetic and copies ran while one was open for 0% -> 0% of each run, Pallas kernels for 17% -> 17%
where the time goes in v2:
time: 279 us; the launch traced here: 278 us
  blocking collectives  161 us (58%)
  Pallas kernels  61.9 us (22%)
  waiting for transfers between devices  26.2 us (9%)
  starting transfers between devices  21.5 us (8%)
  local copies, waits for them, and re-layouts  5.43 us (2%)
    all_to_all x6, blocking collectives, exchange(): lax.all_to_all(pieces, CHIPS, split_axis=0, concat_axis=0, tiled=True)  144 us
    pallas_call x9, Pallas kernels, call(): pl.pallas_call(kernel, out_shape=[jax.ShapeDtypeStruct(s, jnp.float32) fo...  61.9 us
    all_to_all x1, blocking collectives, to_cells(): lax.all_to_all(pieces, BAND, split_axis=0, concat_axis=0, tiled=True)  17.1 us
    ppermute x8, waiting for transfers between devices, swapped(): return lax.ppermute(x, 'band_1', ring(lax.axis_size('band_1'), 1))  8.41 us
    ppermute x3, starting transfers between devices, neighbours(): far = lax.ppermute(v, EVERY, slab_pairs(1))  7.73 us
    all_to_all x1, waiting for transfers between devices, exchange(): lax.all_to_all(pieces, CHIPS, split_axis=0, concat_axis=0, tiled=True)  7.61 us
    all_to_all x1, starting transfers between devices, exchange(): lax.all_to_all(pieces, CHIPS, split_axis=0, concat_axis=0, tiled=True)  6.34 us
  transfers between devices with their start and end apart: 24, of which 9 were waited for; matrix products, arithmetic and copies ran while one was open for 0% of the time, Pallas kernels for 17%

profile of v2, /device:TPU:0, one launch (start us, length us, event | category | flops | bytes accessed | tf_op | source)
XLA Modules:
  0.0 278.2 jit_solution(17136561920388501551)
XLA Ops:
  0.7 1.0 copy-done.1
  1.8 1.0 copy-done.2
  3.5 17.1 %all_to_all.40 = f32[4,2,4,4,16,128]{5,4,3,2,1,0:T(8,128)S(1)} all-to-all(f32[4,2,4,4,16,128]{5,4,3,2,1,0:T(8,128)S(1)} %shard_map.58), channel_id=1, replica_groups=mesh['grid'=32,'band_0'=2,'band_1'=2] {'band_0','band_1'}, dimensions={0} | all-to-all | bytes 2097152 | tf_op jit(solution)/shard_map/all_to_all | solution.py:546
  20.7 1.6 shard_map.59
  22.4 2.4 collective-permute-done
  24.9 27.4 %all_to_all.41 = f32[832,2,128]{2,1,0:T(2,128)S(1)} all-to-all(f32[832,2,128]{2,1,0:T(2,128)S(1)} %bitcast.65), channel_id=1, replica_groups=mesh['grid'=32,'band_0'=2,'band_1'=2] {'grid','band_0'}, dimensions={0} | all-to-all | bytes 1703936 | tf_op jit(solution)/shard_map/all_to_all | solution.py:512
  52.7 20.2 %all_to_all.42 = f32[832,2,128]{2,1,0:T(2,128)S(1)} all-to-all(f32[832,2,128]{2,1,0:T(2,128)S(1)} %bitcast.67), channel_id=1, replica_groups=mesh['grid'=32,'band_0'=2,'band_1'=2] {'grid','band_0'}, dimensions={0} | all-to-all | bytes 1703936 | tf_op jit(solution)/shard_map/all_to_all | solution.py:512
  74.4 2.5 collective-permute-start.2
  77.0 15.1 %shard_map.60.x_ref = f32[512,512]{1,0:T(8,128)S(1)} custom-call(s32[4]{0:T(128)S(1)} %pad_add_fusion.core_ref.refs_0_, f32[1664,128]{1,0:T(8,128)S(1)} %bitcast.49, f32[1664,128]{1,0:T(8,128)S(1)} %collective-permute-done.1.other_ref.in_other_ref), custom_call_target="tpu_custom_call" | custom-call | flops 20000000000 | bytes 1703936 | tf_op jit(solution)/shard_map/pallas_call | solution.py:553
  92.1 2.1 collective-permute-done.2.far_ref
  94.3 4.4 %shard_map.61 = (f32[4,256,128]{2,1,0:T(8,128)S(1)}, f32[4,4,4,16,128]{4,3,2,1,0:T(8,128)S(1)}, f32[2176,128]{1,0:T(8,128)S(1)}, f32[2176,128]{1,0:T(8,128)S(1)}) custom-call(s32[4]{0:T(128)S(1)} %pad_add_fusion.core_ref.refs_0_, f32[512,512]{1,0:T(8,128)S(1)} %shard_map.60.x_ref, f32[1664,128]{1,0:T(8,128)S(1)} %bitcast.50, ...), custom_call_target="tpu_custom_call" | custom-call | flops 2000000000 | bytes 6029312 | tf_op jit(solution)/shard_map/pallas_call | solution.py:553
  99.1 2.5 collective-permute-done.6
  101.8 24.3 %all_to_all.43 = f32[1088,2,128]{2,1,0:T(2,128)S(1)} all-to-all(f32[1088,2,128]{2,1,0:T(2,128)S(1)} %bitcast.59), channel_id=1, replica_groups=mesh['grid'=32,'band_0'=2,'band_1'=2] {'grid','band_0'}, dimensions={0} | all-to-all | bytes 2228224 | tf_op jit(solution)/shard_map/all_to_all | solution.py:512
  126.7 23.5 %all_to_all.44 = f32[1088,2,128]{2,1,0:T(2,128)S(1)} all-to-all(f32[1088,2,128]{2,1,0:T(2,128)S(1)} %bitcast.63), channel_id=1, replica_groups=mesh['grid'=32,'band_0'=2,'band_1'=2] {'grid','band_0'}, dimensions={0} | all-to-all | bytes 2228224 | tf_op jit(solution)/shard_map/all_to_all | solution.py:512
  151.0 0.9 collective-permute-start.9
  151.9 2.6 collective-permute-start.8
  154.5 15.6 %shard_map.62 = (f32[512,512]{1,0:T(8,128)S(1)}, f32[8,128]{1,0:T(8,128)S(1)}) custom-call(s32[4]{0:T(128)S(1)} %pad_add_fusion.core_ref.refs_0_, f32[2176,128]{1,0:T(8,128)S(1)} %bitcast.46, f32[2176,128]{1,0:T(8,128)S(1)} %collective-permute-done.7.other_ref.in_other_ref), custom_call_target="tpu_custom_call" | custom-call | flops 20000000000 | bytes 2228224 | tf_op jit(solution)/shard_map/pallas_call | solution.py:553
  170.1 1.6 collective-permute-done.8.far_ref
  171.7 4.5 %shard_map.63 = (f32[4,256,128]{2,1,0:T(8,128)S(1)}, f32[4,4,4,16,128]{4,3,2,1,0:T(8,128)S(1)}, f32[2176,128]{1,0:T(8,128)S(1)}, f32[2176,128]{1,0:T(8,128)S(1)}) custom-call(s32[4]{0:T(128)S(1)} %pad_add_fusion.core_ref.refs_0_, f32[512,512]{1,0:T(8,128)S(1)} %get-tuple-element.26.x_ref, f32[8,128]{1,0:T(8,128)S(1)} %get-tuple-element.27.stats_ref, ...), custom_call_target="tpu_custom_call" | custom-call | flops 2000000000 | bytes 7081984 | tf_op jit(solution)/shard_map/pallas_call | solution.py:553
  176.5 2.6 collective-permute-done.12
  179.1 24.8 %all_to_all.45 = f32[1088,2,128]{2,1,0:T(2,128)S(1)} all-to-all(f32[1088,2,128]{2,1,0:T(2,128)S(1)} %bitcast.60), channel_id=1, replica_groups=mesh['grid'=32,'band_0'=2,'band_1'=2] {'grid','band_0'}, dimensions={0} | all-to-all | bytes 2228224 | tf_op jit(solution)/shard_map/all_to_all | solution.py:512
  204.6 23.4 %all_to_all.46 = f32[1088,2,128]{2,1,0:T(2,128)S(1)} all-to-all(f32[1088,2,128]{2,1,0:T(2,128)S(1)} %bitcast.64), channel_id=1, replica_groups=mesh['grid'=32,'band_0'=2,'band_1'=2] {'grid','band_0'}, dimensions={0} | all-to-all | bytes 2228224 | tf_op jit(solution)/shard_map/all_to_all | solution.py:512
  229.6 2.6 collective-permute-start.14
  232.2 15.6 %shard_map.64 = (f32[512,512]{1,0:T(8,128)S(1)}, f32[8,128]{1,0:T(8,128)S(1)}) custom-call(s32[4]{0:T(128)S(1)} %pad_add_fusion.core_ref.refs_0_, f32[2176,128]{1,0:T(8,128)S(1)} %bitcast.43, f32[2176,128]{1,0:T(8,128)S(1)} %collective-permute-done.13.other_ref.refs_4_), custom_call_target="tpu_custom_call" | custom-call | flops 20000000000 | bytes 2228224 | tf_op jit(solution)/shard_map/pallas_call | solution.py:553
  247.9 1.6 collective-permute-done.14.refs_7_
  249.4 2.9 %shard_map.65 = (f32[4,2,4,4,16,128]{5,4,3,2,1,0:T(8,128)S(1)}, f32[6,128]{1,0:T(8,128)S(1)}, f32[6,128]{1,0:T(8,128)S(1)}) custom-call(s32[4]{0:T(128)S(1)} %pad_add_fusion.core_ref.refs_0_, f32[512,512]{1,0:T(8,128)S(1)} %get-tuple-element.32.refs_1_, f32[8,128]{1,0:T(8,128)S(1)} %get-tuple-element.33.refs_2_, f32[2176,128]{1,0:T(8,128)S(1)} %bitcast.44, ...), custom_call_target="tpu_custom_call" | custom-call | flops 2000000000 | bytes 7081984 | tf_op jit(solution)/shard_map/pallas_call | solution.py:553
  252.6 1.0 collective-permute-done.21
  254.3 6.3 %all-to-all-start.7 = ((f32[192,2,128]{2,1,0:T(2,128)}), f32[192,2,128]{2,1,0:T(2,128)S(1)}, u32[]{:S(2)}, u32[]{:S(2)}) async-start(f32[192,2,128]{2,1,0:T(2,128)} %bitcast.23), calls=%async_computation.7 | async-start | bytes 393216 | tf_op jit(solution)/shard_map/all_to_all | solution.py:512
  261.5 1.0 collective-permute-start.20
  263.3 7.6 %all-to-all-done.7 = f32[192,2,128]{2,1,0:T(2,128)S(1)} async-done(((f32[192,2,128]{2,1,0:T(2,128)}), f32[192,2,128]{2,1,0:T(2,128)S(1)}, u32[]{:S(2)}, u32[]{:S(2)}) %all-to-all-start.7) | async-done | bytes 196640 | tf_op jit(solution)/shard_map/all_to_all | solution.py:512
  271.2 4.9 %collective-permute-done.19.across_ref = f32[2,4,4,16,128]{4,3,2,1,0:T(8,128)S(1)} collective-permute-done((f32[2,4,4,16,128]{4,3,2,1,0:T(8,128)S(1)}, f32[2,4,4,16,128]{4,3,2,1,0:T(8,128)S(1)}, u32[]{:S(2)}, u32[]{:S(2)}) %collective-permute-start.19) | collective-permute-done | bytes 262176 | tf_op jit(solution)/shard_map/ppermute | solution.py:609
  276.1 1.5 shard_map.66
  (67 shorter events, 11.1 us)
Async XLA Ops:
  0.6 72.3 %copy-start = (f32[4,16,16]{2,1,0:T(8,128)S(1)}, f32[4,16,16]{2,1,0:T(8,128)}, u32[]{:S(2)}) copy-start(f32[4,16,16]{2,1,0:T(8,128)} %param.5) | copy-start | bytes 12292
  0.7 1.0 copy-start.1
  1.8 1.0 copy-start.2
  22.3 2.5 collective-permute-start
  72.9 4.0 %collective-permute-start.1 = (f32[1664,128]{1,0:T(8,128)S(1)}, f32[1664,128]{1,0:T(8,128)S(1)}, u32[]{:S(2)}, u32[]{:S(2)}) collective-permute-start(f32[1664,128]{1,0:T(8,128)S(1)} %bitcast.48), channel_id=1, source_target_pairs={{0,1},{1,0},{2,3},{3,2},{4,5},{5,4},{6,7},{7,6},{8,9},{9,8},{10,11... | collective-permute-start | bytes 2555912 | tf_op jit(solution)/shard_map/ppermute | solution.py:508
  73.0 19.1 %collective-permute-start.5 = (f32[4,4,4,16,128]{4,3,2,1,0:T(8,128)S(1)}, f32[4,4,4,16,128]{4,3,2,1,0:T(8,128)S(1)}, u32[]{:S(2)}, u32[]{:S(2)}) collective-permute-start(f32[4,4,4,16,128]{4,3,2,1,0:T(8,128)S(1)} %get-tuple-element.45.v_ref), channel_id=1, source_target_pairs={{0,3},{1,0},{2,1},{3,2},{4,7},{5,4},{6,5},{7,6},{8,11},{9,8},{10,9... | collective-permute-start | bytes 1572872 | tf_op jit(solution)/shard_map/ppermute | solution.py:504
  73.7 18.4 %collective-permute-start.4 = (f32[4,4,4,16,128]{4,3,2,1,0:T(8,128)S(1)}, f32[4,4,4,16,128]{4,3,2,1,0:T(8,128)S(1)}, u32[]{:S(2)}, u32[]{:S(2)}) collective-permute-start(f32[4,4,4,16,128]{4,3,2,1,0:T(8,128)S(1)} %get-tuple-element.45.v_ref), channel_id=1, source_target_pairs={{0,1},{1,2},{2,3},{3,0},{4,5},{5,6},{6,7},{7,4},{8,9},{9,10},{10,1... | collective-permute-start | bytes 1572872 | tf_op jit(solution)/shard_map/ppermute | solution.py:504
  73.7 18.4 %collective-permute-start.3 = (f32[4,4,4,16,128]{4,3,2,1,0:T(8,128)S(1)}, f32[4,4,4,16,128]{4,3,2,1,0:T(8,128)S(1)}, u32[]{:S(2)}, u32[]{:S(2)}) collective-permute-start(f32[4,4,4,16,128]{4,3,2,1,0:T(8,128)S(1)} %get-tuple-element.45.v_ref), channel_id=1, source_target_pairs={{0,4},{1,5},{2,6},{3,7},{4,0},{5,1},{6,2},{7,3},{8,12},{9,13},{10,... | collective-permute-start | bytes 1572872 | tf_op jit(solution)/shard_map/ppermute | solution.py:503
  74.4 19.8 %collective-permute-start.2 = (f32[4,4,4,16,128]{4,3,2,1,0:T(8,128)S(1)}, f32[4,4,4,16,128]{4,3,2,1,0:T(8,128)S(1)}, u32[]{:S(2)}, u32[]{:S(2)}) collective-permute-start(f32[4,4,4,16,128]{4,3,2,1,0:T(8,128)S(1)} %get-tuple-element.45.v_ref), channel_id=1, source_target_pairs={{0,126},{1,127},{2,124},{3,125},{4,8},{5,9},{6,10},{7,11},{8,4},{9... | collective-permute-start | bytes 1572872 | tf_op jit(solution)/shard_map/ppermute | solution.py:502
  98.8 3.0 %copy-start.3 = (f32[4,4,4,16,128]{4,3,2,1,0:T(8,128)}, f32[4,4,4,16,128]{4,3,2,1,0:T(8,128)S(1)}, u32[]{:S(2)}) copy-start(f32[4,4,4,16,128]{4,3,2,1,0:T(8,128)S(1)} %get-tuple-element.29.v_ref) | copy-start | bytes 1572868
  98.8 3.0 %copy-start.5 = (f32[4,256,128]{2,1,0:T(8,128)}, f32[4,256,128]{2,1,0:T(8,128)S(1)}, u32[]{:S(2)}) copy-start(f32[4,256,128]{2,1,0:T(8,128)S(1)} %get-tuple-element.28.old_ref) | copy-start | bytes 1572868
  98.8 2.8 %collective-permute-start.6 = (f32[2176,128]{1,0:T(8,128)S(1)}, f32[2176,128]{1,0:T(8,128)S(1)}, u32[]{:S(2)}, u32[]{:S(2)}) collective-permute-start(f32[2176,128]{1,0:T(8,128)S(1)} %get-tuple-element.25), channel_id=1, source_target_pairs={{0,1},{1,0},{2,3},{3,2},{4,5},{5,4},{6,7},{7,6},{8,9},{9,8},{10,11... | collective-permute-start | bytes 3342344 | tf_op jit(solution)/shard_map/ppermute | solution.py:508
  126.7 23.5 %copy-start.4 = (f32[4,4,4,16,128]{4,3,2,1,0:T(8,128)S(1)}, f32[4,4,4,16,128]{4,3,2,1,0:T(8,128)}, u32[]{:S(2)}) copy-start(f32[4,4,4,16,128]{4,3,2,1,0:T(8,128)} %copy-done.3) | copy-start | bytes 1572868
  150.3 4.2 %collective-permute-start.7 = (f32[2176,128]{1,0:T(8,128)S(1)}, f32[2176,128]{1,0:T(8,128)S(1)}, u32[]{:S(2)}, u32[]{:S(2)}) collective-permute-start(f32[2176,128]{1,0:T(8,128)S(1)} %bitcast.45), channel_id=1, source_target_pairs={{0,1},{1,0},{2,3},{3,2},{4,5},{5,4},{6,7},{7,6},{8,9},{9,8},{10,11... | collective-permute-start | bytes 3342344 | tf_op jit(solution)/shard_map/ppermute | solution.py:508
  150.3 21.4 %copy-start.6 = (f32[4,256,128]{2,1,0:T(8,128)S(1)}, f32[4,256,128]{2,1,0:T(8,128)}, u32[]{:S(2)}) copy-start(f32[4,256,128]{2,1,0:T(8,128)} %copy-done.5) | copy-start | bytes 1572868
  150.3 19.8 %collective-permute-start.11 = (f32[4,4,4,16,128]{4,3,2,1,0:T(8,128)S(1)}, f32[4,4,4,16,128]{4,3,2,1,0:T(8,128)S(1)}, u32[]{:S(2)}, u32[]{:S(2)}) collective-permute-start(f32[4,4,4,16,128]{4,3,2,1,0:T(8,128)S(1)} %copy-done.4), channel_id=1, source_target_pairs={{0,3},{1,0},{2,1},{3,2},{4,7},{5,4},{6,5},{7,6},{8,11},{9,8},{10,9... | collective-permute-start | bytes 1572872 | tf_op jit(solution)/shard_map/ppermute | solution.py:504
  151.0 19.2 %collective-permute-start.10 = (f32[4,4,4,16,128]{4,3,2,1,0:T(8,128)S(1)}, f32[4,4,4,16,128]{4,3,2,1,0:T(8,128)S(1)}, u32[]{:S(2)}, u32[]{:S(2)}) collective-permute-start(f32[4,4,4,16,128]{4,3,2,1,0:T(8,128)S(1)} %copy-done.4), channel_id=1, source_target_pairs={{0,1},{1,2},{2,3},{3,0},{4,5},{5,6},{6,7},{7,4},{8,9},{9,10},{10,1... | collective-permute-start | bytes 1572872 | tf_op jit(solution)/shard_map/ppermute | solution.py:504
  151.0 19.2 %collective-permute-start.9 = (f32[4,4,4,16,128]{4,3,2,1,0:T(8,128)S(1)}, f32[4,4,4,16,128]{4,3,2,1,0:T(8,128)S(1)}, u32[]{:S(2)}, u32[]{:S(2)}) collective-permute-start(f32[4,4,4,16,128]{4,3,2,1,0:T(8,128)S(1)} %copy-done.4), channel_id=1, source_target_pairs={{0,4},{1,5},{2,6},{3,7},{4,0},{5,1},{6,2},{7,3},{8,12},{9,13},{10,... | collective-permute-start | bytes 1572872 | tf_op jit(solution)/shard_map/ppermute | solution.py:503
  151.9 19.8 %collective-permute-start.8 = (f32[4,4,4,16,128]{4,3,2,1,0:T(8,128)S(1)}, f32[4,4,4,16,128]{4,3,2,1,0:T(8,128)S(1)}, u32[]{:S(2)}, u32[]{:S(2)}) collective-permute-start(f32[4,4,4,16,128]{4,3,2,1,0:T(8,128)S(1)} %copy-done.4), channel_id=1, source_target_pairs={{0,126},{1,127},{2,124},{3,125},{4,8},{5,9},{6,10},{7,11},{8,4},{9... | collective-permute-start | bytes 1572872 | tf_op jit(solution)/shard_map/ppermute | solution.py:502
  176.2 2.8 %collective-permute-start.12 = (f32[2176,128]{1,0:T(8,128)S(1)}, f32[2176,128]{1,0:T(8,128)S(1)}, u32[]{:S(2)}, u32[]{:S(2)}) collective-permute-start(f32[2176,128]{1,0:T(8,128)S(1)} %get-tuple-element.31), channel_id=1, source_target_pairs={{0,1},{1,0},{2,3},{3,2},{4,5},{5,4},{6,7},{7,6},{8,9},{9,8},{10,11... | collective-permute-start | bytes 3342344 | tf_op jit(solution)/shard_map/ppermute | solution.py:508
  228.0 4.2 %collective-permute-start.13 = (f32[2176,128]{1,0:T(8,128)S(1)}, f32[2176,128]{1,0:T(8,128)S(1)}, u32[]{:S(2)}, u32[]{:S(2)}) collective-permute-start(f32[2176,128]{1,0:T(8,128)S(1)} %bitcast.42), channel_id=1, source_target_pairs={{0,1},{1,0},{2,3},{3,2},{4,5},{5,4},{6,7},{7,6},{8,9},{9,8},{10,11... | collective-permute-start | bytes 3342344 | tf_op jit(solution)/shard_map/ppermute | solution.py:508
  228.0 19.8 %collective-permute-start.17 = (f32[4,4,4,16,128]{4,3,2,1,0:T(8,128)S(1)}, f32[4,4,4,16,128]{4,3,2,1,0:T(8,128)S(1)}, u32[]{:S(2)}, u32[]{:S(2)}) collective-permute-start(f32[4,4,4,16,128]{4,3,2,1,0:T(8,128)S(1)} %get-tuple-element.35.refs_6_), channel_id=1, source_target_pairs={{0,3},{1,0},{2,1},{3,2},{4,7},{5,4},{6,5},{7,6},{8,11},{9,8},{10,9... | collective-permute-start | bytes 1572872 | tf_op jit(solution)/shard_map/ppermute | solution.py:504
  228.7 19.2 %collective-permute-start.16 = (f32[4,4,4,16,128]{4,3,2,1,0:T(8,128)S(1)}, f32[4,4,4,16,128]{4,3,2,1,0:T(8,128)S(1)}, u32[]{:S(2)}, u32[]{:S(2)}) collective-permute-start(f32[4,4,4,16,128]{4,3,2,1,0:T(8,128)S(1)} %get-tuple-element.35.refs_6_), channel_id=1, source_target_pairs={{0,1},{1,2},{2,3},{3,0},{4,5},{5,6},{6,7},{7,4},{8,9},{9,10},{10,1... | collective-permute-start | bytes 1572872 | tf_op jit(solution)/shard_map/ppermute | solution.py:504
  228.7 19.2 %collective-permute-start.15 = (f32[4,4,4,16,128]{4,3,2,1,0:T(8,128)S(1)}, f32[4,4,4,16,128]{4,3,2,1,0:T(8,128)S(1)}, u32[]{:S(2)}, u32[]{:S(2)}) collective-permute-start(f32[4,4,4,16,128]{4,3,2,1,0:T(8,128)S(1)} %get-tuple-element.35.refs_6_), channel_id=1, source_target_pairs={{0,4},{1,5},{2,6},{3,7},{4,0},{5,1},{6,2},{7,3},{8,12},{9,13},{10,... | collective-permute-start | bytes 1572872 | tf_op jit(solution)/shard_map/ppermute | solution.py:503
  229.6 19.8 %collective-permute-start.14 = (f32[4,4,4,16,128]{4,3,2,1,0:T(8,128)S(1)}, f32[4,4,4,16,128]{4,3,2,1,0:T(8,128)S(1)}, u32[]{:S(2)}, u32[]{:S(2)}) collective-permute-start(f32[4,4,4,16,128]{4,3,2,1,0:T(8,128)S(1)} %get-tuple-element.35.refs_6_), channel_id=1, source_target_pairs={{0,126},{1,127},{2,124},{3,125},{4,8},{5,9},{6,10},{7,11},{8,4},{9... | collective-permute-start | bytes 1572872 | tf_op jit(solution)/shard_map/ppermute | solution.py:502
  252.4 1.2 collective-permute-start.21
  254.3 16.6 %all-to-all-start.7 = ((f32[192,2,128]{2,1,0:T(2,128)}), f32[192,2,128]{2,1,0:T(2,128)S(1)}, u32[]{:S(2)}, u32[]{:S(2)}) async-start(f32[192,2,128]{2,1,0:T(2,128)} %bitcast.23), calls=%async_computation.7 | async-start | bytes 393216 | tf_op jit(solution)/shard_map/all_to_all | solution.py:512
  261.5 9.7 %collective-permute-start.20 = (f32[2,4,4,16,128]{4,3,2,1,0:T(8,128)}, f32[2,4,4,16,128]{4,3,2,1,0:T(8,128)S(1)}, u32[]{:S(2)}, u32[]{:S(2)}) collective-permute-start(f32[2,4,4,16,128]{4,3,2,1,0:T(8,128)} %get-tuple-element.41), channel_id=1, source_target_pairs={{0,3},{1,0},{2,1},{3,2},{4,7},{5,4},{6,5},{7,6},{8,11},{9,8},{10,9... | collective-permute-start | bytes 786440 | tf_op jit(solution)/shard_map/ppermute | solution.py:609
  262.5 13.6 %collective-permute-start.19 = (f32[2,4,4,16,128]{4,3,2,1,0:T(8,128)S(1)}, f32[2,4,4,16,128]{4,3,2,1,0:T(8,128)S(1)}, u32[]{:S(2)}, u32[]{:S(2)}) collective-permute-start(f32[2,4,4,16,128]{4,3,2,1,0:T(8,128)S(1)} %get-tuple-element.42), channel_id=1, source_target_pairs={{0,2},{1,3},{2,0},{3,1},{4,6},{5,7},{6,4},{7,5},{8,10},{9,11},{10,... | collective-permute-start | bytes 786440 | tf_op jit(solution)/shard_map/ppermute | solution.py:609
  263.2 12.9 %collective-permute-start.18 = (f32[2,4,4,16,128]{4,3,2,1,0:T(8,128)S(1)}, f32[2,4,4,16,128]{4,3,2,1,0:T(8,128)S(1)}, u32[]{:S(2)}, u32[]{:S(2)}) collective-permute-start(f32[2,4,4,16,128]{4,3,2,1,0:T(8,128)S(1)} %get-tuple-element.43), channel_id=1, source_target_pairs={{0,1},{1,2},{2,3},{3,0},{4,5},{5,6},{6,7},{7,4},{8,9},{9,10},{10,1... | collective-permute-start | bytes 786440 | tf_op jit(solution)/shard_map/ppermute | solution.py:609
  271.1 5.0 %collective-permute-start.22 = (f32[64,6,128]{2,1,0:T(8,128)S(1)}, f32[64,6,128]{2,1,0:T(8,128)S(1)}, u32[]{:S(2)}, u32[]{:S(2)}) collective-permute-start(f32[64,6,128]{2,1,0:T(8,128)S(1)} %reshape.74.here_ref), channel_id=1, source_target_pairs={{0,1},{1,0},{2,3},{3,2},{4,5},{5,4},{6,7},{7,6},{8,9},{9,8},{10,11... | collective-permute-start | bytes 589832 | tf_op jit(solution)/shard_map/ppermute | solution.py:508

commit v3 on v2

--- a/solution.py
+++ b/solution.py
@@ -291,15 +291,21 @@
     return jnp.concatenate([rows[at + b : at + b + 1] for b in range(blocks)], axis=1)
 
 
-def last_kernel(core_ref, own_ref, near_ref, across_ref, far_ref, here_ref, there_ref, v_ref, stats_ref):
+def last_kernel(
+    core_ref, own_ref, near_ref, across_ref, far_ref, here_ref, there_ref, *refs,
+):
     planes, rows = own_ref.shape[1:3]
     totals = totals_of(core_ref[0], here_ref, there_ref)
     blocks = totals.shape[0] // 3
     rayleigh, energy, weight = (totals[blocks * k : blocks * (k + 1)] for k in range(3))
+    *earlier, v_ref, quotients_ref, norms_ref, stats_ref = refs
     stats_ref[:blocks, :] = rayleigh
     stats_ref[blocks:, :] = squared_of(rayleigh, energy, weight)
-    rayleigh = stats_ref[pl.ds(core_ref[1], 1), :]
-    length = length_of(stats_ref[pl.ds(blocks + core_ref[1], 1), :])
+    for at, ref in enumerate((*earlier, stats_ref)):
+        rayleigh, squared = (ref[pl.ds(blocks * k + core_ref[1], 1), :] for k in range(2))
+        quotients_ref[at : at + 1, :] = rayleigh
+        norms_ref[at : at + 1, :] = jnp.sqrt(squared)
+    length = length_of(squared)
     for away, ref in enumerate((own_ref, near_ref, across_ref, far_ref)):
         first_row = rows * lax.rem(core_ref[1] + core_ref[2] + blocks - away, blocks)
         for z in range(planes):
@@ -610,13 +616,13 @@
     lines = (mine + swapped(other)).reshape(-1, LINES, lanes)
     here = from_every_chip(lines)
     here = here.reshape(lax.axis_size(CHIPS), *sums)
-    v, stats = call(
-        last_kernel, [(planes, blocks * rows, columns, lanes), stats_shape], *parts, here, swapped(here)
-    )
-    stats_list.append(stats)
-    stats = jnp.stack(stats_list).reshape(ITERS, 2, blocks, lanes)
-    stats = lax.dynamic_slice_in_dim(stats, band, 1, 2)[:, :, 0]
-    return (v, stats[:, 0], jnp.sqrt(stats[:, 1]))
+    lines = (ITERS, lanes)
+    return tuple(
+        call(
+            last_kernel, [(planes, blocks * rows, columns, lanes), lines, lines], *parts, here,
+            swapped(here), *stats_list, scratch=[stats_shape],
+        )
+    )
 
 
 def solution(mesh):

time: 279 us -> 278 us (level)
  no operation moved by 1% of the time
where the time goes in v3:
time: 278 us
  blocking collectives  161 us (58%)
  Pallas kernels  61.9 us (22%)
  waiting for transfers between devices  26.2 us (9%)
  starting transfers between devices  21.5 us (8%)
  local copies, waits for them, and re-layouts  4.84 us (2%)
    all_to_all x6, blocking collectives, exchange(): lax.all_to_all(pieces, CHIPS, split_axis=0, concat_axis=0, tiled=True)  144 us
    pallas_call x9, Pallas kernels, call(): pl.pallas_call(kernel, out_shape=[jax.ShapeDtypeStruct(s, jnp.float32) fo...  61.9 us
    all_to_all x1, blocking collectives, to_cells(): lax.all_to_all(pieces, BAND, split_axis=0, concat_axis=0, tiled=True)  17.1 us
    ppermute x8, waiting for transfers between devices, swapped(): return lax.ppermute(x, 'band_1', ring(lax.axis_size('band_1'), 1))  8.41 us
    ppermute x3, starting transfers between devices, neighbours(): far = lax.ppermute(v, EVERY, slab_pairs(1))  7.73 us
    all_to_all x1, waiting for transfers between devices, exchange(): lax.all_to_all(pieces, CHIPS, split_axis=0, concat_axis=0, tiled=True)  7.61 us
    all_to_all x1, starting transfers between devices, exchange(): lax.all_to_all(pieces, CHIPS, split_axis=0, concat_axis=0, tiled=True)  6.34 us
  transfers between devices with their start and end apart: 24, of which 9 were waited for; matrix products, arithmetic and copies ran while one was open for 0% of the time, Pallas kernels for 17%

profile of v3, /device:TPU:0, one launch (start us, length us, event | category | flops | bytes accessed | tf_op | source)
XLA Modules:
  0.0 277.6 jit_solution(9903954345918964872)
XLA Ops:
  0.7 1.0 copy-done.1
  1.8 1.0 copy-done.2
  3.5 17.1 %all_to_all.40 = f32[4,2,4,4,16,128]{5,4,3,2,1,0:T(8,128)S(1)} all-to-all(f32[4,2,4,4,16,128]{5,4,3,2,1,0:T(8,128)S(1)} %shard_map.58), channel_id=1, replica_groups=mesh['grid'=32,'band_0'=2,'band_1'=2] {'band_0','band_1'}, dimensions={0} | all-to-all | bytes 2097152 | tf_op jit(solution)/shard_map/all_to_all | solution.py:552
  20.7 1.6 shard_map.59
  22.4 2.4 collective-permute-done
  24.9 27.4 %all_to_all.41 = f32[832,2,128]{2,1,0:T(2,128)S(1)} all-to-all(f32[832,2,128]{2,1,0:T(2,128)S(1)} %bitcast.52), channel_id=1, replica_groups=mesh['grid'=32,'band_0'=2,'band_1'=2] {'grid','band_0'}, dimensions={0} | all-to-all | bytes 1703936 | tf_op jit(solution)/shard_map/all_to_all | solution.py:518
  52.7 20.2 %all_to_all.42 = f32[832,2,128]{2,1,0:T(2,128)S(1)} all-to-all(f32[832,2,128]{2,1,0:T(2,128)S(1)} %bitcast.54), channel_id=1, replica_groups=mesh['grid'=32,'band_0'=2,'band_1'=2] {'grid','band_0'}, dimensions={0} | all-to-all | bytes 1703936 | tf_op jit(solution)/shard_map/all_to_all | solution.py:518
  74.4 2.5 collective-permute-start.2
  77.0 15.1 %shard_map.60.x_ref = f32[512,512]{1,0:T(8,128)S(1)} custom-call(s32[4]{0:T(128)S(1)} %pad_add_fusion.core_ref.refs_0_, f32[1664,128]{1,0:T(8,128)S(1)} %bitcast.39, f32[1664,128]{1,0:T(8,128)S(1)} %collective-permute-done.1.other_ref.in_other_ref), custom_call_target="tpu_custom_call" | custom-call | flops 20000000000 | bytes 1703936 | tf_op jit(solution)/shard_map/pallas_call | solution.py:559
  92.1 2.1 collective-permute-done.2.far_ref
  94.3 4.4 %shard_map.61 = (f32[4,256,128]{2,1,0:T(8,128)S(1)}, f32[4,4,4,16,128]{4,3,2,1,0:T(8,128)S(1)}, f32[2176,128]{1,0:T(8,128)S(1)}, f32[2176,128]{1,0:T(8,128)S(1)}) custom-call(s32[4]{0:T(128)S(1)} %pad_add_fusion.core_ref.refs_0_, f32[512,512]{1,0:T(8,128)S(1)} %shard_map.60.x_ref, f32[1664,128]{1,0:T(8,128)S(1)} %bitcast.40, ...), custom_call_target="tpu_custom_call" | custom-call | flops 2000000000 | bytes 6029312 | tf_op jit(solution)/shard_map/pallas_call | solution.py:559
  99.1 2.5 collective-permute-done.6
  101.8 24.3 %all_to_all.43 = f32[1088,2,128]{2,1,0:T(2,128)S(1)} all-to-all(f32[1088,2,128]{2,1,0:T(2,128)S(1)} %bitcast.46), channel_id=1, replica_groups=mesh['grid'=32,'band_0'=2,'band_1'=2] {'grid','band_0'}, dimensions={0} | all-to-all | bytes 2228224 | tf_op jit(solution)/shard_map/all_to_all | solution.py:518
  126.7 23.5 %all_to_all.44 = f32[1088,2,128]{2,1,0:T(2,128)S(1)} all-to-all(f32[1088,2,128]{2,1,0:T(2,128)S(1)} %bitcast.50), channel_id=1, replica_groups=mesh['grid'=32,'band_0'=2,'band_1'=2] {'grid','band_0'}, dimensions={0} | all-to-all | bytes 2228224 | tf_op jit(solution)/shard_map/all_to_all | solution.py:518
  151.0 0.9 collective-permute-start.9
  151.9 2.6 collective-permute-start.8
  154.5 15.6 %shard_map.62 = (f32[512,512]{1,0:T(8,128)S(1)}, f32[8,128]{1,0:T(8,128)S(1)}) custom-call(s32[4]{0:T(128)S(1)} %pad_add_fusion.core_ref.refs_0_, f32[2176,128]{1,0:T(8,128)S(1)} %bitcast.36, f32[2176,128]{1,0:T(8,128)S(1)} %collective-permute-done.7.other_ref.in_other_ref), custom_call_target="tpu_custom_call" | custom-call | flops 20000000000 | bytes 2228224 | tf_op jit(solution)/shard_map/pallas_call | solution.py:559
  170.1 1.6 collective-permute-done.8.far_ref
  171.7 4.5 %shard_map.63 = (f32[4,256,128]{2,1,0:T(8,128)S(1)}, f32[4,4,4,16,128]{4,3,2,1,0:T(8,128)S(1)}, f32[2176,128]{1,0:T(8,128)S(1)}, f32[2176,128]{1,0:T(8,128)S(1)}) custom-call(s32[4]{0:T(128)S(1)} %pad_add_fusion.core_ref.refs_0_, f32[512,512]{1,0:T(8,128)S(1)} %get-tuple-element.24.x_ref, f32[8,128]{1,0:T(8,128)S(1)} %get-tuple-element.25.stats_ref.refs_0_, ...), custom_call_target="tpu_custom_call" | custom-call | flops 2000000000 | bytes 7081984 | tf_op jit(solution)/shard_map/pallas_call | solution.py:559
  176.5 2.6 collective-permute-done.12
  179.1 24.8 %all_to_all.45 = f32[1088,2,128]{2,1,0:T(2,128)S(1)} all-to-all(f32[1088,2,128]{2,1,0:T(2,128)S(1)} %bitcast.47), channel_id=1, replica_groups=mesh['grid'=32,'band_0'=2,'band_1'=2] {'grid','band_0'}, dimensions={0} | all-to-all | bytes 2228224 | tf_op jit(solution)/shard_map/all_to_all | solution.py:518
  204.6 23.4 %all_to_all.46 = f32[1088,2,128]{2,1,0:T(2,128)S(1)} all-to-all(f32[1088,2,128]{2,1,0:T(2,128)S(1)} %bitcast.51), channel_id=1, replica_groups=mesh['grid'=32,'band_0'=2,'band_1'=2] {'grid','band_0'}, dimensions={0} | all-to-all | bytes 2228224 | tf_op jit(solution)/shard_map/all_to_all | solution.py:518
  229.6 2.6 collective-permute-start.14
  232.2 15.6 %shard_map.64 = (f32[512,512]{1,0:T(8,128)S(1)}, f32[8,128]{1,0:T(8,128)S(1)}) custom-call(s32[4]{0:T(128)S(1)} %pad_add_fusion.core_ref.refs_0_, f32[2176,128]{1,0:T(8,128)S(1)} %bitcast.33, f32[2176,128]{1,0:T(8,128)S(1)} %collective-permute-done.13.other_ref.refs_4_), custom_call_target="tpu_custom_call" | custom-call | flops 20000000000 | bytes 2228224 | tf_op jit(solution)/shard_map/pallas_call | solution.py:559
  247.9 1.6 collective-permute-done.14.refs_7_
  249.4 2.9 %shard_map.65 = (f32[4,2,4,4,16,128]{5,4,3,2,1,0:T(8,128)S(1)}, f32[6,128]{1,0:T(8,128)S(1)}, f32[6,128]{1,0:T(8,128)S(1)}) custom-call(s32[4]{0:T(128)S(1)} %pad_add_fusion.core_ref.refs_0_, f32[512,512]{1,0:T(8,128)S(1)} %get-tuple-element.30.refs_1_, f32[8,128]{1,0:T(8,128)S(1)} %get-tuple-element.31.refs_2_.refs_1_, f32[2176,128]{1,0:T(8,128)S(1)} %bitcast.34, ...), custom_call_target="tpu_custom_call" | custom-call | flops 2000000000 | bytes 7081984 | tf_op jit(solution)/shard_map/pallas_call | solution.py:559
  252.6 1.0 collective-permute-done.21
  254.3 6.3 %all-to-all-start.7 = ((f32[192,2,128]{2,1,0:T(2,128)}), f32[192,2,128]{2,1,0:T(2,128)S(1)}, u32[]{:S(2)}, u32[]{:S(2)}) async-start(f32[192,2,128]{2,1,0:T(2,128)} %bitcast.23), calls=%async_computation.7 | async-start | bytes 393216 | tf_op jit(solution)/shard_map/all_to_all | solution.py:518
  261.5 1.0 collective-permute-start.20
  263.3 7.6 %all-to-all-done.7 = f32[192,2,128]{2,1,0:T(2,128)S(1)} async-done(((f32[192,2,128]{2,1,0:T(2,128)}), f32[192,2,128]{2,1,0:T(2,128)S(1)}, u32[]{:S(2)}, u32[]{:S(2)}) %all-to-all-start.7) | async-done | bytes 196640 | tf_op jit(solution)/shard_map/all_to_all | solution.py:518
  271.2 4.9 %collective-permute-done.19.across_ref = f32[2,4,4,16,128]{4,3,2,1,0:T(8,128)S(1)} collective-permute-done((f32[2,4,4,16,128]{4,3,2,1,0:T(8,128)S(1)}, f32[2,4,4,16,128]{4,3,2,1,0:T(8,128)S(1)}, u32[]{:S(2)}, u32[]{:S(2)}) %collective-permute-start.19) | collective-permute-done | bytes 262176 | tf_op jit(solution)/shard_map/ppermute | solution.py:615
  276.1 1.5 shard_map.66
  (64 shorter events, 10.5 us)
Async XLA Ops:
  0.6 72.3 %copy-start = (f32[4,16,16]{2,1,0:T(8,128)S(1)}, f32[4,16,16]{2,1,0:T(8,128)}, u32[]{:S(2)}) copy-start(f32[4,16,16]{2,1,0:T(8,128)} %param.5) | copy-start | bytes 12292
  0.7 1.0 copy-start.1
  1.8 1.0 copy-start.2
  22.3 2.5 collective-permute-start
  72.9 4.0 %collective-permute-start.1 = (f32[1664,128]{1,0:T(8,128)S(1)}, f32[1664,128]{1,0:T(8,128)S(1)}, u32[]{:S(2)}, u32[]{:S(2)}) collective-permute-start(f32[1664,128]{1,0:T(8,128)S(1)} %bitcast.38), channel_id=1, source_target_pairs={{0,1},{1,0},{2,3},{3,2},{4,5},{5,4},{6,7},{7,6},{8,9},{9,8},{10,11... | collective-permute-start | bytes 2555912 | tf_op jit(solution)/shard_map/ppermute | solution.py:514
  73.0 19.1 %collective-permute-start.5 = (f32[4,4,4,16,128]{4,3,2,1,0:T(8,128)S(1)}, f32[4,4,4,16,128]{4,3,2,1,0:T(8,128)S(1)}, u32[]{:S(2)}, u32[]{:S(2)}) collective-permute-start(f32[4,4,4,16,128]{4,3,2,1,0:T(8,128)S(1)} %get-tuple-element.41.v_ref), channel_id=1, source_target_pairs={{0,3},{1,0},{2,1},{3,2},{4,7},{5,4},{6,5},{7,6},{8,11},{9,8},{10,9... | collective-permute-start | bytes 1572872 | tf_op jit(solution)/shard_map/ppermute | solution.py:510
  73.7 18.4 %collective-permute-start.4 = (f32[4,4,4,16,128]{4,3,2,1,0:T(8,128)S(1)}, f32[4,4,4,16,128]{4,3,2,1,0:T(8,128)S(1)}, u32[]{:S(2)}, u32[]{:S(2)}) collective-permute-start(f32[4,4,4,16,128]{4,3,2,1,0:T(8,128)S(1)} %get-tuple-element.41.v_ref), channel_id=1, source_target_pairs={{0,1},{1,2},{2,3},{3,0},{4,5},{5,6},{6,7},{7,4},{8,9},{9,10},{10,1... | collective-permute-start | bytes 1572872 | tf_op jit(solution)/shard_map/ppermute | solution.py:510
  73.7 18.4 %collective-permute-start.3 = (f32[4,4,4,16,128]{4,3,2,1,0:T(8,128)S(1)}, f32[4,4,4,16,128]{4,3,2,1,0:T(8,128)S(1)}, u32[]{:S(2)}, u32[]{:S(2)}) collective-permute-start(f32[4,4,4,16,128]{4,3,2,1,0:T(8,128)S(1)} %get-tuple-element.41.v_ref), channel_id=1, source_target_pairs={{0,4},{1,5},{2,6},{3,7},{4,0},{5,1},{6,2},{7,3},{8,12},{9,13},{10,... | collective-permute-start | bytes 1572872 | tf_op jit(solution)/shard_map/ppermute | solution.py:509
  74.4 19.8 %collective-permute-start.2 = (f32[4,4,4,16,128]{4,3,2,1,0:T(8,128)S(1)}, f32[4,4,4,16,128]{4,3,2,1,0:T(8,128)S(1)}, u32[]{:S(2)}, u32[]{:S(2)}) collective-permute-start(f32[4,4,4,16,128]{4,3,2,1,0:T(8,128)S(1)} %get-tuple-element.41.v_ref), channel_id=1, source_target_pairs={{0,126},{1,127},{2,124},{3,125},{4,8},{5,9},{6,10},{7,11},{8,4},{9... | collective-permute-start | bytes 1572872 | tf_op jit(solution)/shard_map/ppermute | solution.py:508
  98.8 3.0 %copy-start.3 = (f32[4,4,4,16,128]{4,3,2,1,0:T(8,128)}, f32[4,4,4,16,128]{4,3,2,1,0:T(8,128)S(1)}, u32[]{:S(2)}) copy-start(f32[4,4,4,16,128]{4,3,2,1,0:T(8,128)S(1)} %get-tuple-element.27.v_ref) | copy-start | bytes 1572868
  98.8 3.0 %copy-start.5 = (f32[4,256,128]{2,1,0:T(8,128)}, f32[4,256,128]{2,1,0:T(8,128)S(1)}, u32[]{:S(2)}) copy-start(f32[4,256,128]{2,1,0:T(8,128)S(1)} %get-tuple-element.26.old_ref) | copy-start | bytes 1572868
  98.8 2.8 %collective-permute-start.6 = (f32[2176,128]{1,0:T(8,128)S(1)}, f32[2176,128]{1,0:T(8,128)S(1)}, u32[]{:S(2)}, u32[]{:S(2)}) collective-permute-start(f32[2176,128]{1,0:T(8,128)S(1)} %get-tuple-element.23), channel_id=1, source_target_pairs={{0,1},{1,0},{2,3},{3,2},{4,5},{5,4},{6,7},{7,6},{8,9},{9,8},{10,11... | collective-permute-start | bytes 3342344 | tf_op jit(solution)/shard_map/ppermute | solution.py:514
  126.7 23.5 %copy-start.4 = (f32[4,4,4,16,128]{4,3,2,1,0:T(8,128)S(1)}, f32[4,4,4,16,128]{4,3,2,1,0:T(8,128)}, u32[]{:S(2)}) copy-start(f32[4,4,4,16,128]{4,3,2,1,0:T(8,128)} %copy-done.3) | copy-start | bytes 1572868
  150.3 4.2 %collective-permute-start.7 = (f32[2176,128]{1,0:T(8,128)S(1)}, f32[2176,128]{1,0:T(8,128)S(1)}, u32[]{:S(2)}, u32[]{:S(2)}) collective-permute-start(f32[2176,128]{1,0:T(8,128)S(1)} %bitcast.35), channel_id=1, source_target_pairs={{0,1},{1,0},{2,3},{3,2},{4,5},{5,4},{6,7},{7,6},{8,9},{9,8},{10,11... | collective-permute-start | bytes 3342344 | tf_op jit(solution)/shard_map/ppermute | solution.py:514
  150.3 21.4 %copy-start.6 = (f32[4,256,128]{2,1,0:T(8,128)S(1)}, f32[4,256,128]{2,1,0:T(8,128)}, u32[]{:S(2)}) copy-start(f32[4,256,128]{2,1,0:T(8,128)} %copy-done.5) | copy-start | bytes 1572868
  150.3 19.8 %collective-permute-start.11 = (f32[4,4,4,16,128]{4,3,2,1,0:T(8,128)S(1)}, f32[4,4,4,16,128]{4,3,2,1,0:T(8,128)S(1)}, u32[]{:S(2)}, u32[]{:S(2)}) collective-permute-start(f32[4,4,4,16,128]{4,3,2,1,0:T(8,128)S(1)} %copy-done.4), channel_id=1, source_target_pairs={{0,3},{1,0},{2,1},{3,2},{4,7},{5,4},{6,5},{7,6},{8,11},{9,8},{10,9... | collective-permute-start | bytes 1572872 | tf_op jit(solution)/shard_map/ppermute | solution.py:510
  151.0 19.2 %collective-permute-start.10 = (f32[4,4,4,16,128]{4,3,2,1,0:T(8,128)S(1)}, f32[4,4,4,16,128]{4,3,2,1,0:T(8,128)S(1)}, u32[]{:S(2)}, u32[]{:S(2)}) collective-permute-start(f32[4,4,4,16,128]{4,3,2,1,0:T(8,128)S(1)} %copy-done.4), channel_id=1, source_target_pairs={{0,1},{1,2},{2,3},{3,0},{4,5},{5,6},{6,7},{7,4},{8,9},{9,10},{10,1... | collective-permute-start | bytes 1572872 | tf_op jit(solution)/shard_map/ppermute | solution.py:510
  151.0 19.2 %collective-permute-start.9 = (f32[4,4,4,16,128]{4,3,2,1,0:T(8,128)S(1)}, f32[4,4,4,16,128]{4,3,2,1,0:T(8,128)S(1)}, u32[]{:S(2)}, u32[]{:S(2)}) collective-permute-start(f32[4,4,4,16,128]{4,3,2,1,0:T(8,128)S(1)} %copy-done.4), channel_id=1, source_target_pairs={{0,4},{1,5},{2,6},{3,7},{4,0},{5,1},{6,2},{7,3},{8,12},{9,13},{10,... | collective-permute-start | bytes 1572872 | tf_op jit(solution)/shard_map/ppermute | solution.py:509
  151.9 19.8 %collective-permute-start.8 = (f32[4,4,4,16,128]{4,3,2,1,0:T(8,128)S(1)}, f32[4,4,4,16,128]{4,3,2,1,0:T(8,128)S(1)}, u32[]{:S(2)}, u32[]{:S(2)}) collective-permute-start(f32[4,4,4,16,128]{4,3,2,1,0:T(8,128)S(1)} %copy-done.4), channel_id=1, source_target_pairs={{0,126},{1,127},{2,124},{3,125},{4,8},{5,9},{6,10},{7,11},{8,4},{9... | collective-permute-start | bytes 1572872 | tf_op jit(solution)/shard_map/ppermute | solution.py:508
  176.2 2.8 %collective-permute-start.12 = (f32[2176,128]{1,0:T(8,128)S(1)}, f32[2176,128]{1,0:T(8,128)S(1)}, u32[]{:S(2)}, u32[]{:S(2)}) collective-permute-start(f32[2176,128]{1,0:T(8,128)S(1)} %get-tuple-element.29), channel_id=1, source_target_pairs={{0,1},{1,0},{2,3},{3,2},{4,5},{5,4},{6,7},{7,6},{8,9},{9,8},{10,11... | collective-permute-start | bytes 3342344 | tf_op jit(solution)/shard_map/ppermute | solution.py:514
  228.0 4.2 %collective-permute-start.13 = (f32[2176,128]{1,0:T(8,128)S(1)}, f32[2176,128]{1,0:T(8,128)S(1)}, u32[]{:S(2)}, u32[]{:S(2)}) collective-permute-start(f32[2176,128]{1,0:T(8,128)S(1)} %bitcast.32), channel_id=1, source_target_pairs={{0,1},{1,0},{2,3},{3,2},{4,5},{5,4},{6,7},{7,6},{8,9},{9,8},{10,11... | collective-permute-start | bytes 3342344 | tf_op jit(solution)/shard_map/ppermute | solution.py:514
  228.0 19.8 %collective-permute-start.17 = (f32[4,4,4,16,128]{4,3,2,1,0:T(8,128)S(1)}, f32[4,4,4,16,128]{4,3,2,1,0:T(8,128)S(1)}, u32[]{:S(2)}, u32[]{:S(2)}) collective-permute-start(f32[4,4,4,16,128]{4,3,2,1,0:T(8,128)S(1)} %get-tuple-element.33.refs_6_), channel_id=1, source_target_pairs={{0,3},{1,0},{2,1},{3,2},{4,7},{5,4},{6,5},{7,6},{8,11},{9,8},{10,9... | collective-permute-start | bytes 1572872 | tf_op jit(solution)/shard_map/ppermute | solution.py:510
  228.7 19.2 %collective-permute-start.16 = (f32[4,4,4,16,128]{4,3,2,1,0:T(8,128)S(1)}, f32[4,4,4,16,128]{4,3,2,1,0:T(8,128)S(1)}, u32[]{:S(2)}, u32[]{:S(2)}) collective-permute-start(f32[4,4,4,16,128]{4,3,2,1,0:T(8,128)S(1)} %get-tuple-element.33.refs_6_), channel_id=1, source_target_pairs={{0,1},{1,2},{2,3},{3,0},{4,5},{5,6},{6,7},{7,4},{8,9},{9,10},{10,1... | collective-permute-start | bytes 1572872 | tf_op jit(solution)/shard_map/ppermute | solution.py:510
  228.7 19.2 %collective-permute-start.15 = (f32[4,4,4,16,128]{4,3,2,1,0:T(8,128)S(1)}, f32[4,4,4,16,128]{4,3,2,1,0:T(8,128)S(1)}, u32[]{:S(2)}, u32[]{:S(2)}) collective-permute-start(f32[4,4,4,16,128]{4,3,2,1,0:T(8,128)S(1)} %get-tuple-element.33.refs_6_), channel_id=1, source_target_pairs={{0,4},{1,5},{2,6},{3,7},{4,0},{5,1},{6,2},{7,3},{8,12},{9,13},{10,... | collective-permute-start | bytes 1572872 | tf_op jit(solution)/shard_map/ppermute | solution.py:509
  229.6 19.8 %collective-permute-start.14 = (f32[4,4,4,16,128]{4,3,2,1,0:T(8,128)S(1)}, f32[4,4,4,16,128]{4,3,2,1,0:T(8,128)S(1)}, u32[]{:S(2)}, u32[]{:S(2)}) collective-permute-start(f32[4,4,4,16,128]{4,3,2,1,0:T(8,128)S(1)} %get-tuple-element.33.refs_6_), channel_id=1, source_target_pairs={{0,126},{1,127},{2,124},{3,125},{4,8},{5,9},{6,10},{7,11},{8,4},{9... | collective-permute-start | bytes 1572872 | tf_op jit(solution)/shard_map/ppermute | solution.py:508
  252.4 1.2 collective-permute-start.21
  254.3 16.6 %all-to-all-start.7 = ((f32[192,2,128]{2,1,0:T(2,128)}), f32[192,2,128]{2,1,0:T(2,128)S(1)}, u32[]{:S(2)}, u32[]{:S(2)}) async-start(f32[192,2,128]{2,1,0:T(2,128)} %bitcast.23), calls=%async_computation.7 | async-start | bytes 393216 | tf_op jit(solution)/shard_map/all_to_all | solution.py:518
  261.5 9.7 %collective-permute-start.20 = (f32[2,4,4,16,128]{4,3,2,1,0:T(8,128)}, f32[2,4,4,16,128]{4,3,2,1,0:T(8,128)S(1)}, u32[]{:S(2)}, u32[]{:S(2)}) collective-permute-start(f32[2,4,4,16,128]{4,3,2,1,0:T(8,128)} %get-tuple-element.37), channel_id=1, source_target_pairs={{0,3},{1,0},{2,1},{3,2},{4,7},{5,4},{6,5},{7,6},{8,11},{9,8},{10,9... | collective-permute-start | bytes 786440 | tf_op jit(solution)/shard_map/ppermute | solution.py:615
  262.5 13.6 %collective-permute-start.19 = (f32[2,4,4,16,128]{4,3,2,1,0:T(8,128)S(1)}, f32[2,4,4,16,128]{4,3,2,1,0:T(8,128)S(1)}, u32[]{:S(2)}, u32[]{:S(2)}) collective-permute-start(f32[2,4,4,16,128]{4,3,2,1,0:T(8,128)S(1)} %get-tuple-element.38), channel_id=1, source_target_pairs={{0,2},{1,3},{2,0},{3,1},{4,6},{5,7},{6,4},{7,5},{8,10},{9,11},{10,... | collective-permute-start | bytes 786440 | tf_op jit(solution)/shard_map/ppermute | solution.py:615
  263.2 12.9 %collective-permute-start.18 = (f32[2,4,4,16,128]{4,3,2,1,0:T(8,128)S(1)}, f32[2,4,4,16,128]{4,3,2,1,0:T(8,128)S(1)}, u32[]{:S(2)}, u32[]{:S(2)}) collective-permute-start(f32[2,4,4,16,128]{4,3,2,1,0:T(8,128)S(1)} %get-tuple-element.39), channel_id=1, source_target_pairs={{0,1},{1,2},{2,3},{3,0},{4,5},{5,6},{6,7},{7,4},{8,9},{9,10},{10,1... | collective-permute-start | bytes 786440 | tf_op jit(solution)/shard_map/ppermute | solution.py:615
  271.1 5.0 %collective-permute-start.22 = (f32[64,6,128]{2,1,0:T(8,128)S(1)}, f32[64,6,128]{2,1,0:T(8,128)S(1)}, u32[]{:S(2)}, u32[]{:S(2)}) collective-permute-start(f32[64,6,128]{2,1,0:T(8,128)S(1)} %reshape.66.here_ref), channel_id=1, source_target_pairs={{0,1},{1,0},{2,3},{3,2},{4,5},{5,4},{6,7},{7,6},{8,9},{9,8},{10,11... | collective-permute-start | bytes 589832 | tf_op jit(solution)/shard_map/ppermute | solution.py:514

commit v4 on v3

--- a/solution.py
+++ b/solution.py
@@ -535,20 +535,28 @@
 
 
 def pieces_kernel(core_ref, first_ref, second_ref, out_ref):
-    quarters, _, planes, rows, _, _ = out_ref.shape
+    quarters, _, _, rows, _, _ = out_ref.shape
     for q in range(quarters):
-        first_row = rows * lax.rem(core_ref[2] + q, quarters)
+        first_row = rows * lax.rem(core_ref[0] + q, quarters)
         for k, ref in enumerate((first_ref, second_ref)):
-            for z in range(planes):
-                for x in range(rows):
-                    out_ref[q, k, z, x] = ref[z, first_row + x]
+            for x in range(rows):
+                out_ref[q, k, 0, x] = ref[0, first_row + x]
 
 
 def to_cells(first, second):
     quarters = lax.axis_size(BAND)
     z, x, y, lanes = first.shape
-    shape = (quarters, 2, z, x // quarters, y, lanes)
-    (pieces,) = call(pieces_kernel, [shape], first, second, flops=1_000_000)
+    rows = x // quarters
+    plane = pl.BlockSpec((1, x, y, lanes), lambda at: (at, 0, 0, 0))
+    pieces = pl.pallas_call(
+        pieces_kernel,
+        grid=(z,),
+        out_shape=jax.ShapeDtypeStruct((quarters, 2, z, rows, y, lanes), jnp.float32),
+        in_specs=[pl.BlockSpec(memory_space=pltpu.SMEM), plane, plane],
+        out_specs=pl.BlockSpec((quarters, 2, 1, rows, y, lanes), lambda at: (0, 0, at, 0, 0, 0)),
+        compiler_params=pltpu.CompilerParams(vmem_limit_bytes=60 << 20),
+        name="pieces_kernel",
+    )(turn().astype(jnp.int32).reshape(1), first, second)
     pieces = lax.all_to_all(pieces, BAND, split_axis=0, concat_axis=0, tiled=True)
     return pieces[:, 0], pieces[:, 1]
 

time: 278 us -> 280 us (level)
  blocking collectives: 161 us -> 144 us
  waiting for transfers between devices: 26.2 us -> 40.5 us
  starting transfers between devices: 21.5 us -> 25 us
  Pallas kernels: 61.9 us -> 64.7 us
    all_to_all x1 -> x0, blocking collectives: 17.1 us -> none  [to_cells(): lax.all_to_all(pieces, BAND, split_axis=0, concat_axis=0, tiled=True)]
    all_to_all x0 -> x1, waiting for transfers between devices: none -> 14.3 us  [to_cells(): lax.all_to_all(pieces, BAND, split_axis=0, concat_axis=0, tiled=True)]
    all_to_all x0 -> x1, starting transfers between devices: none -> 3.51 us  [to_cells(): lax.all_to_all(pieces, BAND, split_axis=0, concat_axis=0, tiled=True)]
    pallas_call x0 -> x1, Pallas kernels: none -> 3.41 us  [to_cells(): pl.pallas_call(pieces_kernel, grid=(z,), out_shape=jax.ShapeDtypeStruct((...]
    pallas_call x9 -> x8, Pallas kernels: 61.9 us -> 61.3 us  [call(): pl.pallas_call(kernel, out_shape=[jax.ShapeDtypeStruct(s, jnp.float32) fo...]
  transfers between devices with their start and end apart: 24 -> 25, of which waited for: 9 -> 10; matrix products, arithmetic and copies ran while one was open for 0% -> 0% of each run, Pallas kernels for 17% -> 17%
where the time goes in v4:
time: 280 us; the launch traced here: 279 us
  blocking collectives  144 us (51%)
  Pallas kernels  64.7 us (23%)
  waiting for transfers between devices  40.5 us (14%)
  starting transfers between devices  25 us (9%)
    all_to_all x6, blocking collectives, exchange(): lax.all_to_all(pieces, CHIPS, split_axis=0, concat_axis=0, tiled=True)  144 us
    pallas_call x8, Pallas kernels, call(): pl.pallas_call(kernel, out_shape=[jax.ShapeDtypeStruct(s, jnp.float32) fo...  61.3 us
    all_to_all x1, waiting for transfers between devices, to_cells(): lax.all_to_all(pieces, BAND, split_axis=0, concat_axis=0, tiled=True)  14.3 us
    ppermute x8, waiting for transfers between devices, swapped(): return lax.ppermute(x, 'band_1', ring(lax.axis_size('band_1'), 1))  8.41 us
    ppermute x3, starting transfers between devices, neighbours(): far = lax.ppermute(v, EVERY, slab_pairs(1))  7.73 us
    all_to_all x1, waiting for transfers between devices, exchange(): lax.all_to_all(pieces, CHIPS, split_axis=0, concat_axis=0, tiled=True)  7.61 us
    all_to_all x1, starting transfers between devices, exchange(): lax.all_to_all(pieces, CHIPS, split_axis=0, concat_axis=0, tiled=True)  6.34 us
  transfers between devices with their start and end apart: 25, of which 10 were waited for; matrix products, arithmetic and copies ran while one was open for 0% of the time, Pallas kernels for 17%

profile of v4, /device:TPU:0, one launch (start us, length us, event | category | flops | bytes accessed | tf_op | source)
XLA Modules:
  0.0 279.3 jit_solution(14054014439666859497)
XLA Ops:
  0.7 3.4 %pieces_kernel.1 = f32[4,2,4,4,16,128]{5,4,3,2,1,0:T(8,128)} custom-call(s32[1]{0:T(128)} %bitcast.2.core_ref, f32[4,16,16,128]{3,2,1,0:T(8,128)} %first_ref.1, f32[4,16,16,128]{3,2,1,0:T(8,128)} %second_ref.1), custom_call_target="tpu_custom_call" | custom-call | tf_op jit(solution)/shard_map/pieces_kernel/pallas_call | solution.py:551
  4.1 3.5 %all-to-all-start = ((f32[4,2,4,4,16,128]{5,4,3,2,1,0:T(8,128)}), f32[4,2,4,4,16,128]{5,4,3,2,1,0:T(8,128)S(1)}, u32[]{:S(2)}, u32[]{:S(2)}) async-start(f32[4,2,4,4,16,128]{5,4,3,2,1,0:T(8,128)} %pieces_kernel.1), calls=%async_computation | async-start | bytes 2097152 | tf_op jit(solution)/shard_map/all_to_all | solution.py:560
  7.7 14.3 %all-to-all-done = f32[4,2,4,4,16,128]{5,4,3,2,1,0:T(8,128)S(1)} async-done(((f32[4,2,4,4,16,128]{5,4,3,2,1,0:T(8,128)}), f32[4,2,4,4,16,128]{5,4,3,2,1,0:T(8,128)S(1)}, u32[]{:S(2)}, u32[]{:S(2)}) %all-to-all-start) | async-done | bytes 1048608 | tf_op jit(solution)/shard_map/all_to_all | solution.py:560
  22.1 1.6 shard_map.58
  23.8 2.4 collective-permute-done
  26.3 27.6 %all_to_all.40 = f32[832,2,128]{2,1,0:T(2,128)S(1)} all-to-all(f32[832,2,128]{2,1,0:T(2,128)S(1)} %bitcast.52), channel_id=1, replica_groups=mesh['grid'=32,'band_0'=2,'band_1'=2] {'grid','band_0'}, dimensions={0} | all-to-all | bytes 1703936 | tf_op jit(solution)/shard_map/all_to_all | solution.py:518
  54.4 20.2 %all_to_all.41 = f32[832,2,128]{2,1,0:T(2,128)S(1)} all-to-all(f32[832,2,128]{2,1,0:T(2,128)S(1)} %bitcast.54), channel_id=1, replica_groups=mesh['grid'=32,'band_0'=2,'band_1'=2] {'grid','band_0'}, dimensions={0} | all-to-all | bytes 1703936 | tf_op jit(solution)/shard_map/all_to_all | solution.py:518
  76.1 2.5 collective-permute-start.2
  78.6 15.1 %shard_map.59.x_ref = f32[512,512]{1,0:T(8,128)S(1)} custom-call(s32[4]{0:T(128)S(1)} %pad_add_fusion.core_ref.refs_0_, f32[1664,128]{1,0:T(8,128)S(1)} %bitcast.39, f32[1664,128]{1,0:T(8,128)S(1)} %collective-permute-done.1.other_ref.in_other_ref), custom_call_target="tpu_custom_call" | custom-call | flops 20000000000 | bytes 1703936 | tf_op jit(solution)/shard_map/pallas_call | solution.py:567
  93.8 2.1 collective-permute-done.2.far_ref
  96.0 4.4 %shard_map.60 = (f32[4,256,128]{2,1,0:T(8,128)S(1)}, f32[4,4,4,16,128]{4,3,2,1,0:T(8,128)S(1)}, f32[2176,128]{1,0:T(8,128)S(1)}, f32[2176,128]{1,0:T(8,128)S(1)}) custom-call(s32[4]{0:T(128)S(1)} %pad_add_fusion.core_ref.refs_0_, f32[512,512]{1,0:T(8,128)S(1)} %shard_map.59.x_ref, f32[1664,128]{1,0:T(8,128)S(1)} %bitcast.40, ...), custom_call_target="tpu_custom_call" | custom-call | flops 2000000000 | bytes 6029312 | tf_op jit(solution)/shard_map/pallas_call | solution.py:567
  100.8 2.5 collective-permute-done.6
  103.4 24.3 %all_to_all.42 = f32[1088,2,128]{2,1,0:T(2,128)S(1)} all-to-all(f32[1088,2,128]{2,1,0:T(2,128)S(1)} %bitcast.46), channel_id=1, replica_groups=mesh['grid'=32,'band_0'=2,'band_1'=2] {'grid','band_0'}, dimensions={0} | all-to-all | bytes 2228224 | tf_op jit(solution)/shard_map/all_to_all | solution.py:518
  128.4 23.5 %all_to_all.43 = f32[1088,2,128]{2,1,0:T(2,128)S(1)} all-to-all(f32[1088,2,128]{2,1,0:T(2,128)S(1)} %bitcast.50), channel_id=1, replica_groups=mesh['grid'=32,'band_0'=2,'band_1'=2] {'grid','band_0'}, dimensions={0} | all-to-all | bytes 2228224 | tf_op jit(solution)/shard_map/all_to_all | solution.py:518
  153.5 2.6 collective-permute-start.8
  156.1 15.6 %shard_map.61 = (f32[512,512]{1,0:T(8,128)S(1)}, f32[8,128]{1,0:T(8,128)S(1)}) custom-call(s32[4]{0:T(128)S(1)} %pad_add_fusion.core_ref.refs_0_, f32[2176,128]{1,0:T(8,128)S(1)} %bitcast.36, f32[2176,128]{1,0:T(8,128)S(1)} %collective-permute-done.7.other_ref.in_other_ref), custom_call_target="tpu_custom_call" | custom-call | flops 20000000000 | bytes 2228224 | tf_op jit(solution)/shard_map/pallas_call | solution.py:567
  171.8 1.6 collective-permute-done.8.far_ref
  173.4 4.5 %shard_map.62 = (f32[4,256,128]{2,1,0:T(8,128)S(1)}, f32[4,4,4,16,128]{4,3,2,1,0:T(8,128)S(1)}, f32[2176,128]{1,0:T(8,128)S(1)}, f32[2176,128]{1,0:T(8,128)S(1)}) custom-call(s32[4]{0:T(128)S(1)} %pad_add_fusion.core_ref.refs_0_, f32[512,512]{1,0:T(8,128)S(1)} %get-tuple-element.24.x_ref, f32[8,128]{1,0:T(8,128)S(1)} %get-tuple-element.25.stats_ref.refs_0_, ...), custom_call_target="tpu_custom_call" | custom-call | flops 2000000000 | bytes 7081984 | tf_op jit(solution)/shard_map/pallas_call | solution.py:567
  178.1 2.6 collective-permute-done.12
  180.8 24.8 %all_to_all.44 = f32[1088,2,128]{2,1,0:T(2,128)S(1)} all-to-all(f32[1088,2,128]{2,1,0:T(2,128)S(1)} %bitcast.47), channel_id=1, replica_groups=mesh['grid'=32,'band_0'=2,'band_1'=2] {'grid','band_0'}, dimensions={0} | all-to-all | bytes 2228224 | tf_op jit(solution)/shard_map/all_to_all | solution.py:518
  206.3 23.4 %all_to_all.45 = f32[1088,2,128]{2,1,0:T(2,128)S(1)} all-to-all(f32[1088,2,128]{2,1,0:T(2,128)S(1)} %bitcast.51), channel_id=1, replica_groups=mesh['grid'=32,'band_0'=2,'band_1'=2] {'grid','band_0'}, dimensions={0} | all-to-all | bytes 2228224 | tf_op jit(solution)/shard_map/all_to_all | solution.py:518
  230.4 0.9 collective-permute-start.15
  231.3 2.6 collective-permute-start.14
  233.9 15.6 %shard_map.63 = (f32[512,512]{1,0:T(8,128)S(1)}, f32[8,128]{1,0:T(8,128)S(1)}) custom-call(s32[4]{0:T(128)S(1)} %pad_add_fusion.core_ref.refs_0_, f32[2176,128]{1,0:T(8,128)S(1)} %bitcast.33, f32[2176,128]{1,0:T(8,128)S(1)} %collective-permute-done.13.other_ref.refs_4_), custom_call_target="tpu_custom_call" | custom-call | flops 20000000000 | bytes 2228224 | tf_op jit(solution)/shard_map/pallas_call | solution.py:567
  249.5 1.6 collective-permute-done.14.refs_7_
  251.1 2.9 %shard_map.64 = (f32[4,2,4,4,16,128]{5,4,3,2,1,0:T(8,128)S(1)}, f32[6,128]{1,0:T(8,128)S(1)}, f32[6,128]{1,0:T(8,128)S(1)}) custom-call(s32[4]{0:T(128)S(1)} %pad_add_fusion.core_ref.refs_0_, f32[512,512]{1,0:T(8,128)S(1)} %get-tuple-element.30.refs_1_, f32[8,128]{1,0:T(8,128)S(1)} %get-tuple-element.31.refs_2_.refs_1_, f32[2176,128]{1,0:T(8,128)S(1)} %bitcast.34, ...), custom_call_target="tpu_custom_call" | custom-call | flops 2000000000 | bytes 7081984 | tf_op jit(solution)/shard_map/pallas_call | solution.py:567
  254.3 1.0 collective-permute-done.21
  256.0 6.3 %all-to-all-start.7 = ((f32[192,2,128]{2,1,0:T(2,128)}), f32[192,2,128]{2,1,0:T(2,128)S(1)}, u32[]{:S(2)}, u32[]{:S(2)}) async-start(f32[192,2,128]{2,1,0:T(2,128)} %bitcast.23), calls=%async_computation.7 | async-start | bytes 393216 | tf_op jit(solution)/shard_map/all_to_all | solution.py:518
  263.2 1.0 collective-permute-start.20
  265.0 7.6 %all-to-all-done.7 = f32[192,2,128]{2,1,0:T(2,128)S(1)} async-done(((f32[192,2,128]{2,1,0:T(2,128)}), f32[192,2,128]{2,1,0:T(2,128)S(1)}, u32[]{:S(2)}, u32[]{:S(2)}) %all-to-all-start.7) | async-done | bytes 196640 | tf_op jit(solution)/shard_map/all_to_all | solution.py:518
  272.8 4.9 %collective-permute-done.19.across_ref = f32[2,4,4,16,128]{4,3,2,1,0:T(8,128)S(1)} collective-permute-done((f32[2,4,4,16,128]{4,3,2,1,0:T(8,128)S(1)}, f32[2,4,4,16,128]{4,3,2,1,0:T(8,128)S(1)}, u32[]{:S(2)}, u32[]{:S(2)}) %collective-permute-start.19) | collective-permute-done | bytes 262176 | tf_op jit(solution)/shard_map/ppermute | solution.py:623
  277.8 1.5 shard_map.65
  (61 shorter events, 9.8 us)
Async XLA Ops:
  0.6 74.0 %copy-start = (f32[4,16,16]{2,1,0:T(8,128)S(1)}, f32[4,16,16]{2,1,0:T(8,128)}, u32[]{:S(2)}) copy-start(f32[4,16,16]{2,1,0:T(8,128)} %param.5) | copy-start | bytes 12292
  4.1 17.9 %all-to-all-start = ((f32[4,2,4,4,16,128]{5,4,3,2,1,0:T(8,128)}), f32[4,2,4,4,16,128]{5,4,3,2,1,0:T(8,128)S(1)}, u32[]{:S(2)}, u32[]{:S(2)}) async-start(f32[4,2,4,4,16,128]{5,4,3,2,1,0:T(8,128)} %pieces_kernel.1), calls=%async_computation | async-start | bytes 2097152 | tf_op jit(solution)/shard_map/all_to_all | solution.py:560
  23.7 2.5 collective-permute-start
  74.6 4.0 %collective-permute-start.1 = (f32[1664,128]{1,0:T(8,128)S(1)}, f32[1664,128]{1,0:T(8,128)S(1)}, u32[]{:S(2)}, u32[]{:S(2)}) collective-permute-start(f32[1664,128]{1,0:T(8,128)S(1)} %bitcast.38), channel_id=1, source_target_pairs={{0,1},{1,0},{2,3},{3,2},{4,5},{5,4},{6,7},{7,6},{8,9},{9,8},{10,11... | collective-permute-start | bytes 2555912 | tf_op jit(solution)/shard_map/ppermute | solution.py:514
  74.6 19.1 %collective-permute-start.5 = (f32[4,4,4,16,128]{4,3,2,1,0:T(8,128)S(1)}, f32[4,4,4,16,128]{4,3,2,1,0:T(8,128)S(1)}, u32[]{:S(2)}, u32[]{:S(2)}) collective-permute-start(f32[4,4,4,16,128]{4,3,2,1,0:T(8,128)S(1)} %get-tuple-element.41.v_ref), channel_id=1, source_target_pairs={{0,3},{1,0},{2,1},{3,2},{4,7},{5,4},{6,5},{7,6},{8,11},{9,8},{10,9... | collective-permute-start | bytes 1572872 | tf_op jit(solution)/shard_map/ppermute | solution.py:510
  75.4 18.4 %collective-permute-start.4 = (f32[4,4,4,16,128]{4,3,2,1,0:T(8,128)S(1)}, f32[4,4,4,16,128]{4,3,2,1,0:T(8,128)S(1)}, u32[]{:S(2)}, u32[]{:S(2)}) collective-permute-start(f32[4,4,4,16,128]{4,3,2,1,0:T(8,128)S(1)} %get-tuple-element.41.v_ref), channel_id=1, source_target_pairs={{0,1},{1,2},{2,3},{3,0},{4,5},{5,6},{6,7},{7,4},{8,9},{9,10},{10,1... | collective-permute-start | bytes 1572872 | tf_op jit(solution)/shard_map/ppermute | solution.py:510
  75.4 18.4 %collective-permute-start.3 = (f32[4,4,4,16,128]{4,3,2,1,0:T(8,128)S(1)}, f32[4,4,4,16,128]{4,3,2,1,0:T(8,128)S(1)}, u32[]{:S(2)}, u32[]{:S(2)}) collective-permute-start(f32[4,4,4,16,128]{4,3,2,1,0:T(8,128)S(1)} %get-tuple-element.41.v_ref), channel_id=1, source_target_pairs={{0,4},{1,5},{2,6},{3,7},{4,0},{5,1},{6,2},{7,3},{8,12},{9,13},{10,... | collective-permute-start | bytes 1572872 | tf_op jit(solution)/shard_map/ppermute | solution.py:509
  76.1 19.8 %collective-permute-start.2 = (f32[4,4,4,16,128]{4,3,2,1,0:T(8,128)S(1)}, f32[4,4,4,16,128]{4,3,2,1,0:T(8,128)S(1)}, u32[]{:S(2)}, u32[]{:S(2)}) collective-permute-start(f32[4,4,4,16,128]{4,3,2,1,0:T(8,128)S(1)} %get-tuple-element.41.v_ref), channel_id=1, source_target_pairs={{0,126},{1,127},{2,124},{3,125},{4,8},{5,9},{6,10},{7,11},{8,4},{9... | collective-permute-start | bytes 1572872 | tf_op jit(solution)/shard_map/ppermute | solution.py:508
  100.4 3.0 %copy-start.1 = (f32[4,4,4,16,128]{4,3,2,1,0:T(8,128)}, f32[4,4,4,16,128]{4,3,2,1,0:T(8,128)S(1)}, u32[]{:S(2)}) copy-start(f32[4,4,4,16,128]{4,3,2,1,0:T(8,128)S(1)} %get-tuple-element.27.v_ref) | copy-start | bytes 1572868
  100.4 3.0 %copy-start.3 = (f32[4,256,128]{2,1,0:T(8,128)}, f32[4,256,128]{2,1,0:T(8,128)S(1)}, u32[]{:S(2)}) copy-start(f32[4,256,128]{2,1,0:T(8,128)S(1)} %get-tuple-element.26.old_ref) | copy-start | bytes 1572868
  100.5 2.8 %collective-permute-start.6 = (f32[2176,128]{1,0:T(8,128)S(1)}, f32[2176,128]{1,0:T(8,128)S(1)}, u32[]{:S(2)}, u32[]{:S(2)}) collective-permute-start(f32[2176,128]{1,0:T(8,128)S(1)} %get-tuple-element.23), channel_id=1, source_target_pairs={{0,1},{1,0},{2,3},{3,2},{4,5},{5,4},{6,7},{7,6},{8,9},{9,8},{10,11... | collective-permute-start | bytes 3342344 | tf_op jit(solution)/shard_map/ppermute | solution.py:514
  128.4 23.5 %copy-start.2 = (f32[4,4,4,16,128]{4,3,2,1,0:T(8,128)S(1)}, f32[4,4,4,16,128]{4,3,2,1,0:T(8,128)}, u32[]{:S(2)}) copy-start(f32[4,4,4,16,128]{4,3,2,1,0:T(8,128)} %copy-done.1) | copy-start | bytes 1572868
  151.9 4.2 %collective-permute-start.7 = (f32[2176,128]{1,0:T(8,128)S(1)}, f32[2176,128]{1,0:T(8,128)S(1)}, u32[]{:S(2)}, u32[]{:S(2)}) collective-permute-start(f32[2176,128]{1,0:T(8,128)S(1)} %bitcast.35), channel_id=1, source_target_pairs={{0,1},{1,0},{2,3},{3,2},{4,5},{5,4},{6,7},{7,6},{8,9},{9,8},{10,11... | collective-permute-start | bytes 3342344 | tf_op jit(solution)/shard_map/ppermute | solution.py:514
  151.9 21.4 %copy-start.4 = (f32[4,256,128]{2,1,0:T(8,128)S(1)}, f32[4,256,128]{2,1,0:T(8,128)}, u32[]{:S(2)}) copy-start(f32[4,256,128]{2,1,0:T(8,128)} %copy-done.3) | copy-start | bytes 1572868
  152.0 19.8 %collective-permute-start.11 = (f32[4,4,4,16,128]{4,3,2,1,0:T(8,128)S(1)}, f32[4,4,4,16,128]{4,3,2,1,0:T(8,128)S(1)}, u32[]{:S(2)}, u32[]{:S(2)}) collective-permute-start(f32[4,4,4,16,128]{4,3,2,1,0:T(8,128)S(1)} %copy-done.2), channel_id=1, source_target_pairs={{0,3},{1,0},{2,1},{3,2},{4,7},{5,4},{6,5},{7,6},{8,11},{9,8},{10,9... | collective-permute-start | bytes 1572872 | tf_op jit(solution)/shard_map/ppermute | solution.py:510
  152.6 19.2 %collective-permute-start.10 = (f32[4,4,4,16,128]{4,3,2,1,0:T(8,128)S(1)}, f32[4,4,4,16,128]{4,3,2,1,0:T(8,128)S(1)}, u32[]{:S(2)}, u32[]{:S(2)}) collective-permute-start(f32[4,4,4,16,128]{4,3,2,1,0:T(8,128)S(1)} %copy-done.2), channel_id=1, source_target_pairs={{0,1},{1,2},{2,3},{3,0},{4,5},{5,6},{6,7},{7,4},{8,9},{9,10},{10,1... | collective-permute-start | bytes 1572872 | tf_op jit(solution)/shard_map/ppermute | solution.py:510
  152.6 19.2 %collective-permute-start.9 = (f32[4,4,4,16,128]{4,3,2,1,0:T(8,128)S(1)}, f32[4,4,4,16,128]{4,3,2,1,0:T(8,128)S(1)}, u32[]{:S(2)}, u32[]{:S(2)}) collective-permute-start(f32[4,4,4,16,128]{4,3,2,1,0:T(8,128)S(1)} %copy-done.2), channel_id=1, source_target_pairs={{0,4},{1,5},{2,6},{3,7},{4,0},{5,1},{6,2},{7,3},{8,12},{9,13},{10,... | collective-permute-start | bytes 1572872 | tf_op jit(solution)/shard_map/ppermute | solution.py:509
  153.5 19.8 %collective-permute-start.8 = (f32[4,4,4,16,128]{4,3,2,1,0:T(8,128)S(1)}, f32[4,4,4,16,128]{4,3,2,1,0:T(8,128)S(1)}, u32[]{:S(2)}, u32[]{:S(2)}) collective-permute-start(f32[4,4,4,16,128]{4,3,2,1,0:T(8,128)S(1)} %copy-done.2), channel_id=1, source_target_pairs={{0,126},{1,127},{2,124},{3,125},{4,8},{5,9},{6,10},{7,11},{8,4},{9... | collective-permute-start | bytes 1572872 | tf_op jit(solution)/shard_map/ppermute | solution.py:508
  177.9 2.8 %collective-permute-start.12 = (f32[2176,128]{1,0:T(8,128)S(1)}, f32[2176,128]{1,0:T(8,128)S(1)}, u32[]{:S(2)}, u32[]{:S(2)}) collective-permute-start(f32[2176,128]{1,0:T(8,128)S(1)} %get-tuple-element.29), channel_id=1, source_target_pairs={{0,1},{1,0},{2,3},{3,2},{4,5},{5,4},{6,7},{7,6},{8,9},{9,8},{10,11... | collective-permute-start | bytes 3342344 | tf_op jit(solution)/shard_map/ppermute | solution.py:514
  229.7 4.2 %collective-permute-start.13 = (f32[2176,128]{1,0:T(8,128)S(1)}, f32[2176,128]{1,0:T(8,128)S(1)}, u32[]{:S(2)}, u32[]{:S(2)}) collective-permute-start(f32[2176,128]{1,0:T(8,128)S(1)} %bitcast.32), channel_id=1, source_target_pairs={{0,1},{1,0},{2,3},{3,2},{4,5},{5,4},{6,7},{7,6},{8,9},{9,8},{10,11... | collective-permute-start | bytes 3342344 | tf_op jit(solution)/shard_map/ppermute | solution.py:514
  229.7 19.8 %collective-permute-start.17 = (f32[4,4,4,16,128]{4,3,2,1,0:T(8,128)S(1)}, f32[4,4,4,16,128]{4,3,2,1,0:T(8,128)S(1)}, u32[]{:S(2)}, u32[]{:S(2)}) collective-permute-start(f32[4,4,4,16,128]{4,3,2,1,0:T(8,128)S(1)} %get-tuple-element.33.refs_6_), channel_id=1, source_target_pairs={{0,3},{1,0},{2,1},{3,2},{4,7},{5,4},{6,5},{7,6},{8,11},{9,8},{10,9... | collective-permute-start | bytes 1572872 | tf_op jit(solution)/shard_map/ppermute | solution.py:510
  230.4 19.2 %collective-permute-start.16 = (f32[4,4,4,16,128]{4,3,2,1,0:T(8,128)S(1)}, f32[4,4,4,16,128]{4,3,2,1,0:T(8,128)S(1)}, u32[]{:S(2)}, u32[]{:S(2)}) collective-permute-start(f32[4,4,4,16,128]{4,3,2,1,0:T(8,128)S(1)} %get-tuple-element.33.refs_6_), channel_id=1, source_target_pairs={{0,1},{1,2},{2,3},{3,0},{4,5},{5,6},{6,7},{7,4},{8,9},{9,10},{10,1... | collective-permute-start | bytes 1572872 | tf_op jit(solution)/shard_map/ppermute | solution.py:510
  230.4 19.2 %collective-permute-start.15 = (f32[4,4,4,16,128]{4,3,2,1,0:T(8,128)S(1)}, f32[4,4,4,16,128]{4,3,2,1,0:T(8,128)S(1)}, u32[]{:S(2)}, u32[]{:S(2)}) collective-permute-start(f32[4,4,4,16,128]{4,3,2,1,0:T(8,128)S(1)} %get-tuple-element.33.refs_6_), channel_id=1, source_target_pairs={{0,4},{1,5},{2,6},{3,7},{4,0},{5,1},{6,2},{7,3},{8,12},{9,13},{10,... | collective-permute-start | bytes 1572872 | tf_op jit(solution)/shard_map/ppermute | solution.py:509
  231.3 19.8 %collective-permute-start.14 = (f32[4,4,4,16,128]{4,3,2,1,0:T(8,128)S(1)}, f32[4,4,4,16,128]{4,3,2,1,0:T(8,128)S(1)}, u32[]{:S(2)}, u32[]{:S(2)}) collective-permute-start(f32[4,4,4,16,128]{4,3,2,1,0:T(8,128)S(1)} %get-tuple-element.33.refs_6_), channel_id=1, source_target_pairs={{0,126},{1,127},{2,124},{3,125},{4,8},{5,9},{6,10},{7,11},{8,4},{9... | collective-permute-start | bytes 1572872 | tf_op jit(solution)/shard_map/ppermute | solution.py:508
  254.0 1.2 collective-permute-start.21
  256.0 16.6 %all-to-all-start.7 = ((f32[192,2,128]{2,1,0:T(2,128)}), f32[192,2,128]{2,1,0:T(2,128)S(1)}, u32[]{:S(2)}, u32[]{:S(2)}) async-start(f32[192,2,128]{2,1,0:T(2,128)} %bitcast.23), calls=%async_computation.7 | async-start | bytes 393216 | tf_op jit(solution)/shard_map/all_to_all | solution.py:518
  263.2 9.7 %collective-permute-start.20 = (f32[2,4,4,16,128]{4,3,2,1,0:T(8,128)}, f32[2,4,4,16,128]{4,3,2,1,0:T(8,128)S(1)}, u32[]{:S(2)}, u32[]{:S(2)}) collective-permute-start(f32[2,4,4,16,128]{4,3,2,1,0:T(8,128)} %get-tuple-element.37), channel_id=1, source_target_pairs={{0,3},{1,0},{2,1},{3,2},{4,7},{5,4},{6,5},{7,6},{8,11},{9,8},{10,9... | collective-permute-start | bytes 786440 | tf_op jit(solution)/shard_map/ppermute | solution.py:623
  264.1 13.6 %collective-permute-start.19 = (f32[2,4,4,16,128]{4,3,2,1,0:T(8,128)S(1)}, f32[2,4,4,16,128]{4,3,2,1,0:T(8,128)S(1)}, u32[]{:S(2)}, u32[]{:S(2)}) collective-permute-start(f32[2,4,4,16,128]{4,3,2,1,0:T(8,128)S(1)} %get-tuple-element.38), channel_id=1, source_target_pairs={{0,2},{1,3},{2,0},{3,1},{4,6},{5,7},{6,4},{7,5},{8,10},{9,11},{10,... | collective-permute-start | bytes 786440 | tf_op jit(solution)/shard_map/ppermute | solution.py:623
  264.9 12.9 %collective-permute-start.18 = (f32[2,4,4,16,128]{4,3,2,1,0:T(8,128)S(1)}, f32[2,4,4,16,128]{4,3,2,1,0:T(8,128)S(1)}, u32[]{:S(2)}, u32[]{:S(2)}) collective-permute-start(f32[2,4,4,16,128]{4,3,2,1,0:T(8,128)S(1)} %get-tuple-element.39), channel_id=1, source_target_pairs={{0,1},{1,2},{2,3},{3,0},{4,5},{5,6},{6,7},{7,4},{8,9},{9,10},{10,1... | collective-permute-start | bytes 786440 | tf_op jit(solution)/shard_map/ppermute | solution.py:623
  272.7 5.0 %collective-permute-start.22 = (f32[64,6,128]{2,1,0:T(8,128)S(1)}, f32[64,6,128]{2,1,0:T(8,128)S(1)}, u32[]{:S(2)}, u32[]{:S(2)}) collective-permute-start(f32[64,6,128]{2,1,0:T(8,128)S(1)} %reshape.67.here_ref), channel_id=1, source_target_pairs={{0,1},{1,0},{2,3},{3,2},{4,5},{5,4},{6,7},{7,6},{8,9},{9,8},{10,11... | collective-permute-start | bytes 589832 | tf_op jit(solution)/shard_map/ppermute | solution.py:514
